TPU v7x, 256 devices: a whole 4x4x8 slice. The times are simulated.
256 devices in a mesh: shot: 4 (over y_lo, core), space: 64 (over x, z, y_hi).
Axes of the slice: x: 4, y: 4 (y_hi: 2, y_lo: 2; y = y_hi * 2 + y_lo), z: 8, core: 2. Of those that a mesh axis runs over, the one named last changes fastest.
Arguments:
- adjoint_now: float32 [4, 1024, 64, 512], P('shot', 'space'), may hold values from -6 to 6
- adjoint_later: float32 [4, 1024, 64, 512], P('shot', 'space'), may hold values from -6 to 6
- courant: float32 [1024, 64, 512], P('space'), may hold values from 0.05 to 0.2
- checkpoint_codes: int32 [4, 6, 1024, 64, 128], P('shot', None, 'space'), may hold values from -2147483648 to 2147483646
- scale_index: int32 [4, 6, 1024, 256], P('shot', None, 'space'), may hold values from 0 to 63
- scale_table: float32 [64], replicated, may hold values from 0.001 to 0.01
- receiver_cell: int32 [4, 16384], P('shot', 'space'), may hold values from 0 to 33554431, as said below
- observed: float32 [4, 4, 16384], P('shot', None, 'space'), may hold values from -12 to 12
- source_cell: int32 [4, 3], P('shot'), may hold values from 0 to 1023, as said below
Outputs:
- gradient: float32 [1024, 64, 512], P('space', 'shot')
- adjoint_first: float32 [4, 1024, 64, 512], P('shot', 'space')
- adjoint_second: float32 [4, 1024, 64, 512], P('shot', 'space')
- misfit: float32 [], replicated
Inputs may be any that keep to these rules, and one draw needn't show every extreme that they name: `receiver_cell`: for every r, entries r * 256 to (r + 1) * 256 - 1 of each shot's row are flat indices (z * 64 + y) * 512 + x of cells with r * 16 <= z < (r + 1) * 16. `source_cell`: column 0 is a z index below 1024, column 1 a y index below 64, column 2 an x index below 512.
All inputs are finite; a program needn't handle non-finite values.
Results may differ from a plain program's by a relative error of at most 0.0001.
Values sent between devices are 32-bit elements; how exact they have to be, the bound alone decides.
A program may use at most 128 MiB of HBM per device.

v0:
```python
import functools

import jax
import jax.numpy as jnp
from jax import lax
from jax.sharding import Mesh
from jax.sharding import PartitionSpec as P

ITERS = 4
QBLOCK = 128
MUTE = 8
SPACE = ("space_0", "space_1", "space_2")
SHOT = ("shot_0", "shot_1")
SHOT_SPACE = ("shot_0", "shot_1", "space_0", "space_1", "space_2")


COEFFS = (-205.0 / 72.0, 8.0 / 5.0, -1.0 / 5.0, 8.0 / 315.0, -1.0 / 560.0)


def with_halo(block, sides, width):
    for axis, dim in sides:
        count = lax.axis_size(axis)
        forward = [(i, i + 1) for i in range(count - 1)]
        backward = [(target, source) for source, target in forward]
        low = lax.ppermute(
            lax.slice_in_dim(block, block.shape[dim] - width, None, axis=dim), axis, forward
        )
        high = lax.ppermute(lax.slice_in_dim(block, 0, width, axis=dim), axis, backward)
        block = jnp.concatenate([low, block, high], axis=dim)
    return block


def split_up(x, dim, count):
    lengths = x.shape
    tiles = x.reshape(*lengths[:dim], count, lengths[dim] // count, *lengths[dim + 1 :])
    return jnp.moveaxis(tiles, dim, 0)


def sum_at_owner(x, axis, dim):
    tiles = split_up(x, dim, lax.axis_size(axis))
    arrived = lax.all_to_all(tiles, axis, split_axis=0, concat_axis=0, tiled=True)
    return arrived.sum(axis=0)


def by_axis(x, axes):
    return functools.reduce(lax.psum, axes, x)


def decode(words, index, table):
    planes = [jnp.bitwise_and(jnp.right_shift(words, 8 * m), 255) for m in range(4)]
    codes = jnp.concatenate(planes, axis=-1)
    centred = (codes - 128).astype(jnp.float32)
    depth, rows, cols = centred.shape
    onehot = index[..., None] == jnp.arange(table.shape[0], dtype=jnp.int32)
    scale = jnp.sum(jnp.where(onehot, table, 0.0), axis=-1)
    blocks = centred.reshape(depth, rows, cols // QBLOCK, QBLOCK) * scale.reshape(
        depth, rows, cols // QBLOCK, 1
    )
    return blocks.reshape(depth, rows, cols)


def laplace(field):
    depth, rows, cols = field.shape
    deep = with_halo(field, ((SPACE, 0),), 4)
    flat = jnp.pad(field, ((0, 0), (4, 4), (4, 4)))
    total = 3.0 * COEFFS[0] * field
    for step in range(1, 5):
        total = total + COEFFS[step] * (
            deep[4 + step : 4 + step + depth] + deep[4 - step : 4 - step + depth]
        )
        total = total + COEFFS[step] * (
            flat[:, 4 + step : 4 + step + rows, 4 : 4 + cols]
            + flat[:, 4 - step : 4 - step + rows, 4 : 4 + cols]
        )
        total = total + COEFFS[step] * (
            flat[:, 4 : 4 + rows, 4 + step : 4 + step + cols]
            + flat[:, 4 : 4 + rows, 4 - step : 4 - step + cols]
        )
    return total


def body(
    adjoint_now,
    adjoint_later,
    courant,
    checkpoint_codes,
    scale_index,
    scale_table,
    receiver_cell,
    observed,
    source_cell,
):
    now = adjoint_now[0]
    later = adjoint_later[0]
    depth, rows, cols = now.shape
    first_z = lax.axis_index(SPACE) * depth
    cells = receiver_cell[0] - first_z * (rows * cols)
    fields = [
        decode(checkpoint_codes[0, level], scale_index[0, level], scale_table)
        for level in range(ITERS + 2)
    ]
    image = jnp.zeros((depth, rows, cols), jnp.float32)
    misfit_part = jnp.zeros((), jnp.float32)
    for step in range(ITERS):
        level = ITERS - step
        synthetic = jnp.take(fields[level].reshape(-1), cells)
        residual = synthetic - observed[0, level - 1]
        misfit_part = misfit_part + jnp.sum(residual * residual)
        image = image + now * (fields[level + 1] - 2.0 * fields[level] + fields[level - 1])
        stepped = 2.0 * now - later + courant * laplace(now)
        stepped = stepped.reshape(-1).at[cells].add(residual).reshape(depth, rows, cols)
        later = now
        now = stepped
    source = source_cell[0]
    zpos = (first_z + jnp.arange(depth, dtype=jnp.int32)).reshape(depth, 1, 1)
    ypos = jnp.arange(rows, dtype=jnp.int32).reshape(1, rows, 1)
    xpos = jnp.arange(cols, dtype=jnp.int32).reshape(1, 1, cols)
    dist = ((zpos - source[0]) ** 2 + (ypos - source[1]) ** 2 + (xpos - source[2]) ** 2).astype(
        jnp.float32
    )
    muted = image * (1.0 - jnp.exp(-dist / (2.0 * MUTE * MUTE)))
    gradient = sum_at_owner(muted, SHOT, 1)
    count = lax.axis_size(SHOT) * ITERS * receiver_cell.shape[1] * lax.axis_size(SPACE)
    misfit = 0.5 * by_axis(misfit_part, SHOT_SPACE) / count
    return (gradient, now[None], later[None], misfit)


def solution(mesh):
    torus = Mesh(
        mesh.devices.reshape(2, 2, 4, 8, 2), ("shot_0", "shot_1", "space_0", "space_1", "space_2")
    )
    return jax.shard_map(
        body,
        mesh=torus,
        in_specs=(
            P(SHOT, SPACE, None, None),
            P(SHOT, SPACE, None, None),
            P(SPACE, None, None),
            P(SHOT, None, SPACE, None, None),
            P(SHOT, None, SPACE, None),
            P(),
            P(SHOT, SPACE),
            P(SHOT, None, SPACE),
            P(SHOT, None),
        ),
        out_specs=(
            P(SPACE, SHOT, None),
            P(SHOT, SPACE, None, None),
            P(SHOT, SPACE, None, None),
            P(),
        ),
        check_vma=False,
    )
```

profile of v0, /device:TPU:2, one launch (start us, length us, event | category | flops | bytes accessed | tf_op | source)
XLA Modules:
  0.0 297.8 jit_solution(8375104143982420160)
XLA Ops:
  0.6 2.3 slice_bitcast_fusion.1
  2.9 5.1 %collective-permute-start.1 = (f32[4,64,512]{2,1,0:T(8,128)}, f32[4,64,512]{2,1,0:T(8,128)}, u32[]{:S(2)}, u32[]{:S(2)}) collective-permute-start(f32[4,64,512]{2,1,0:T(8,128)} %get-tuple-element.58), channel_id=1, source_target_pairs={{0,1},{1,2},{2,3},{3,4},{4,5},{5,6},{6,7},{7,8},{8,9},{9,10},{10,1... | collective-permute-start | bytes 1572872 | tf_op jit(solution)/shard_map/ppermute | solution.py:25
  8.0 7.2 %collective-permute-start = (f32[4,64,512]{2,1,0:T(8,128)}, f32[4,64,512]{2,1,0:T(8,128)}, u32[]{:S(2)}, u32[]{:S(2)}) collective-permute-start(f32[4,64,512]{2,1,0:T(8,128)} %get-tuple-element.57), channel_id=1, source_target_pairs={{1,0},{2,1},{3,2},{4,3},{5,4},{6,5},{7,6},{8,7},{9,8},{10,9},{11,1... | collective-permute-start | bytes 1572872 | tf_op jit(solution)/shard_map/ppermute | solution.py:28
  15.2 5.1 %and_bitcast_fusion.23 = (s32[16,64,1,128]{3,1,0,2:T(8,128)S(1)}, s32[16,64,1,128]{3,1,0,2:T(8,128)S(1)}, s32[16,64,1,128]{3,1,0,2:T(8,128)}, s32[16,64,1,128]{3...) fusion(s32[1,6,16,64,128]{4,3,2,1,0:T(8,128)} %param.14), kind=kLoop, calls=%fused_computation.301 | loop fusion | flops 4980736 | bytes 13107200 | tf_op jit(solution)/shard_map/and | solution.py:50
  20.4 1.6 and_bitcast_fusion.7
  22.0 1.5 select_reduce_fusion.5
  23.8 4.6 %fusion.155 = (f32[16,64,4,128]{3,1,0,2:T(8,128)S(1)}, f32[16,64,4,128]{3,1,0,2:T(8,128)}) fusion(s32[16,64,1,128]{3,1,0,2:T(8,128)S(1)} %get-tuple-element.36, s32[16,64,1,128]{3,1,0,2:T(8,128)S(1)} %get-tuple-element.35, s32[16,64,1,128]{3,1,0,2:T(8,128)S(1)} %get-tuple-element.34, s32[16,64,1,128]{3,1,0,2:T(8,128)} %get-tuple-element.40, ...), kind=kLoop, calls=%fused_computation.258 | loop fusion | flops 6291456 | bytes 8421376 | tf_op jit(solution)/shard_map/mul | solution.py:56
  28.5 1.4 copy.62
  30.3 5.1 %fusion.151 = (f32[16,64,4,128]{3,1,0,2:T(8,128)S(1)}, f32[16,64,4,128]{3,1,0,2:T(8,128)}) fusion(s32[16,64,1,128]{3,1,0,2:T(8,128)} %get-tuple-element.30, s32[16,64,1,128]{3,1,0,2:T(8,128)} %get-tuple-element.29, s32[16,64,1,128]{3,1,0,2:T(8,128)} %get-tuple-element.28, s32[16,64,1,128]{3,1,0,2:T(8,128)} %get-tuple-element.42, f32[16,64,4]{1,0,2:T(8,128)S(1)} %copy.53, ...), kind=kLoop, calls=%fused_computation.252 | loop fusion | flops 6291456 | bytes 8421376 | tf_op jit(solution)/shard_map/mul | solution.py:56
  35.4 2.7 copy.54
  38.5 5.2 %fusion.147 = (f32[16,64,4,128]{3,1,0,2:T(8,128)}, f32[16,64,4,128]{3,1,0,2:T(8,128)}) fusion(s32[16,64,1,128]{3,1,0,2:T(8,128)} %get-tuple-element.24, s32[16,64,1,128]{3,1,0,2:T(8,128)} %get-tuple-element.23, s32[16,64,1,128]{3,1,0,2:T(8,128)S(1)} %get-tuple-element.22, s32[16,64,1,128]{3,1,0,2:T(8,128)S(1)} %get-tuple-element.21, ...), kind=kLoop, calls=%fused_computation.246 | loop fusion | flops 6291456 | bytes 8421376 | tf_op jit(solution)/shard_map/mul | solution.py:56
  43.8 1.7 gather_fusion.3
  45.5 3.2 %gather_fusion.1 = f32[256]{0:T(256)S(1)} fusion(f32[524288]{0:T(1024)} %bitcast.107, s32[1024]{0:T(1024)S(1)} %pad_clamp_fusion), kind=kCustom, calls=%fused_computation.1.clone | custom fusion | bytes 3072 | tf_op jit(solution)/shard_map/jit(_take)/gather | solution.py:106
  48.7 3.0 %copy.58 = f32[16,64,4,128]{3,2,1,0:T(4,128)S(1)} copy(f32[16,64,4,128]{3,1,0,2:T(8,128)} %get-tuple-element.81) | data formatting | bytes 4194304 | tf_op jit(solution)/shard_map/mul | solution.py:56
  51.7 1.7 gather_fusion.2
  53.5 4.5 %copy.51 = f32[16,64,4,128]{3,2,1,0:T(4,128)} copy(f32[16,64,4,128]{3,1,0,2:T(8,128)} %get-tuple-element.79) | data formatting | bytes 4194304 | tf_op jit(solution)/shard_map/mul | solution.py:56
  58.0 3.5 %gather_fusion = f32[256]{0:T(256)S(1)} fusion(f32[524288]{0:T(1024)} %bitcast.108, s32[1024]{0:T(1024)S(1)} %pad_clamp_fusion), kind=kCustom, calls=%fused_computation.clone | custom fusion | bytes 3072 | tf_op jit(solution)/shard_map/jit(_take)/gather | solution.py:106
  62.2 28.5 %fusion.10 = f32[16,64,512]{2,1,0:T(8,128)S(1)} fusion(f32[16,64,512]{2,1,0:T(8,128)S(1)} %copy-done.4, f32[16,64,512]{2,1,0:T(8,128)} %bitcast.104, f32[4,64,512]{2,1,0:T(8,128)} %collective-permute-done.1, f32[4,64,512]{2,1,0:T(8,128)} %collective-permute-done, f32[1,16,64,512]{3,2,1,0:T(8,128)} %param.12), kind=kLoop, calls=%fused_computation.94 | loop fusion | flops 25690112 | bytes 9437184 | tf_op jit(solution)/shard_map/add | solution.py:110
  91.2 2.9 scatter_fusion
  94.2 1.1 slice.517
  95.3 1.9 collective-permute-start.3
  97.3 8.4 %collective-permute-start.2 = (f32[4,64,512]{2,1,0:T(8,128)S(1)}, f32[4,64,512]{2,1,0:T(8,128)S(1)}, u32[]{:S(2)}, u32[]{:S(2)}) collective-permute-start(f32[4,64,512]{2,1,0:T(8,128)S(1)} %slice.514), channel_id=1, source_target_pairs={{1,0},{2,1},{3,2},{4,3},{5,4},{6,5},{7,6},{8,7},{9,8},{10,9},{11,1... | collective-permute-start | bytes 1572872 | tf_op jit(solution)/shard_map/ppermute | solution.py:28
  108.3 13.3 %psum.35 = f32[]{:T(128)} all-reduce(f32[]{:T(128)S(6)} %add.589), channel_id=1, replica_groups=mesh['shot_0'=2,'shot_1'=2,'space_0'=4,'space_1'=8,'space_2'=2] {'shot_0'}, use_global_device_ids=true, to_apply=%region_15.17 | all-reduce | flops 1 | bytes 8 | tf_op jit(solution)/shard_map/psum | solution.py:46
  121.6 3.1 %psum.36 = f32[]{:T(128)} all-reduce(f32[]{:T(128)} %psum.35), channel_id=1, replica_groups=mesh['shot_0'=2,'shot_1'=2,'space_0'=4,'space_1'=8,'space_2'=2] {'shot_1'}, use_global_device_ids=true, to_apply=%region_16.18 | all-reduce | flops 1 | bytes 8 | tf_op jit(solution)/shard_map/psum | solution.py:46
  124.6 9.2 %psum.37 = f32[]{:T(128)} all-reduce(f32[]{:T(128)} %psum.36), channel_id=1, replica_groups=mesh['shot_0'=2,'shot_1'=2,'space_0'=4,'space_1'=8,'space_2'=2] {'space_0'}, use_global_device_ids=true, to_apply=%region_17.19 | all-reduce | flops 1 | bytes 8 | tf_op jit(solution)/shard_map/psum | solution.py:46
  133.9 18.3 %psum.38 = f32[]{:T(128)} all-reduce(f32[]{:T(128)} %psum.37), channel_id=1, replica_groups=mesh['shot_0'=2,'shot_1'=2,'space_0'=4,'space_1'=8,'space_2'=2] {'space_1'}, use_global_device_ids=true, to_apply=%region_18.20 | all-reduce | flops 1 | bytes 8 | tf_op jit(solution)/shard_map/psum | solution.py:46
  152.2 7.1 %psum.39 = f32[]{:T(128)} all-reduce(f32[]{:T(128)} %psum.38), channel_id=1, replica_groups=mesh['shot_0'=2,'shot_1'=2,'space_0'=4,'space_1'=8,'space_2'=2] {'space_2'}, use_global_device_ids=true, to_apply=%region_19.21 | all-reduce | flops 1 | bytes 8 | tf_op jit(solution)/shard_map/psum | solution.py:46
  159.3 3.2 %mul.383 = f32[16,4,16,512]{3,2,1,0:T(8,128)} reshape(f32[16,64,4,128]{3,2,1,0:T(4,128)} %copy-done.15) | data formatting | bytes 4194304 | tf_op jit(solution)/shard_map/mul | solution.py:56
  162.5 1.9 mul.405
  164.4 3.2 %mul.358 = f32[16,4,16,512]{3,2,1,0:T(8,128)} reshape(f32[16,64,4,128]{3,2,1,0:T(4,128)} %copy.54) | data formatting | bytes 4194304 | tf_op jit(solution)/shard_map/mul | solution.py:56
  167.6 1.8 mul.353
  169.4 3.0 %copy.66 = f32[16,64,4,128]{3,2,1,0:T(4,128)S(1)} copy(f32[16,64,4,128]{3,1,0,2:T(8,128)} %get-tuple-element.83) | data formatting | bytes 4194304 | tf_op jit(solution)/shard_map/mul | solution.py:56
  172.4 1.9 mul.427
  174.3 3.0 %copy.48 = f32[16,64,4,128]{3,2,1,0:T(4,128)S(1)} copy(f32[16,64,4,128]{3,1,0,2:T(8,128)} %get-tuple-element.78) | data formatting | bytes 4194304 | tf_op jit(solution)/shard_map/mul | solution.py:56
  177.3 1.9 mul.349
  180.5 1.7 reshape.630
  182.2 1.5 constant_dynamic-update-slice_fusion.3
  186.0 4.9 %fusion.56 = f32[16,64,512]{2,1,0:T(8,128)S(1)} fusion(f32[16,64,512]{2,1,0:T(8,128)S(1)} %copy-done.5, f32[16,64,512]{2,1,0:T(8,128)S(1)} %reshape.630, f32[20,64,512]{2,1,0:T(8,128)S(1)} %get-tuple-element.56, f32[20,64,512]{2,1,0:T(8,128)S(1)} %constant_dynamic-update-slice_fusion, f32[1,16,64,512]{3,2,1,0:T(8,128)S(1)} %copy-done.10), kind=kLoop, calls=%fused_computation.140 | loop fusion | flops 21495808 | bytes 25165824 | tf_op jit(solution)/shard_map/add | solution.py:110
  190.8 1.9 copy.70
  192.7 4.8 %scatter_fusion.1 = f32[524288]{0:T(1024)} fusion(f32[524288]{0:T(1024)} %bitcast.59, s32[256]{0:T(256)S(1)} %bitcast.122, f32[256]{0:T(256)S(1)} %get-tuple-element.70), kind=kCustom, calls=%fused_computation.5 | custom fusion | flops 256 | bytes 4096 | tf_op jit(solution)/shard_map/scatter-add | solution.py:111
  197.5 1.4 fusion.159
  199.8 5.7 %collective-permute-start.5 = (f32[4,64,512]{2,1,0:T(8,128)}, f32[4,64,512]{2,1,0:T(8,128)S(1)}, u32[]{:S(2)}, u32[]{:S(2)}) collective-permute-start(f32[4,64,512]{2,1,0:T(8,128)} %slice.548), channel_id=1, source_target_pairs={{0,1},{1,2},{2,3},{3,4},{4,5},{5,6},{6,7},{7,8},{8,9},{9,10},{10,1... | collective-permute-start | bytes 1572872 | tf_op jit(solution)/shard_map/ppermute | solution.py:25
  208.3 5.1 %collective-permute-start.4 = (f32[4,64,512]{2,1,0:T(8,128)}, f32[4,64,512]{2,1,0:T(8,128)S(1)}, u32[]{:S(2)}, u32[]{:S(2)}) collective-permute-start(f32[4,64,512]{2,1,0:T(8,128)} %slice.545), channel_id=1, source_target_pairs={{1,0},{2,1},{3,2},{4,3},{5,4},{6,5},{7,6},{8,7},{9,8},{10,9},{11,1... | collective-permute-start | bytes 1572872 | tf_op jit(solution)/shard_map/ppermute | solution.py:28
  213.5 1.5 reshape.629
  215.1 1.7 reshape.633
  216.8 3.5 %reshape.632 = f32[16,4,16,512]{3,2,1,0:T(8,128)} reshape(f32[524288]{0:T(1024)} %scatter_fusion.1) | data formatting | bytes 4194304 | tf_op jit(solution)/shard_map/reshape | solution.py:111
  220.3 2.0 collective-permute-done.5
  222.9 2.5 collective-permute-done.4
  225.4 4.9 %fusion.85 = f32[16,64,512]{2,1,0:T(8,128)S(1)} fusion(f32[16,64,512]{2,1,0:T(8,128)S(1)} %copy-done.6, f32[16,64,512]{2,1,0:T(8,128)S(1)} %reshape.633, f32[20,64,512]{2,1,0:T(8,128)S(1)} %get-tuple-element.52, f32[20,64,512]{2,1,0:T(8,128)S(1)} %constant_dynamic-update-slice_fusion.4, f32[16,64,512]{2,1,0:T(8,128)S(1)} %copy-done.3), kind=kLoop, calls=%fused_computation.169 | loop fusion | flops 21495808 | bytes 25165824 | tf_op jit(solution)/shard_map/add | solution.py:110
  230.9 2.7 scatter_fusion.2
  233.6 1.5 reshape.635
  236.0 4.9 %collective-permute-start.7 = (f32[4,64,512]{2,1,0:T(8,128)}, f32[4,64,512]{2,1,0:T(8,128)}, u32[]{:S(2)}, u32[]{:S(2)}) collective-permute-start(f32[4,64,512]{2,1,0:T(8,128)} %slice.582), channel_id=1, source_target_pairs={{0,1},{1,2},{2,3},{3,4},{4,5},{5,6},{6,7},{7,8},{8,9},{9,10},{10,1... | collective-permute-start | bytes 1572872 | tf_op jit(solution)/shard_map/ppermute | solution.py:25
  241.0 6.3 %collective-permute-start.6 = (f32[4,64,512]{2,1,0:T(8,128)S(1)}, f32[4,64,512]{2,1,0:T(8,128)S(1)}, u32[]{:S(2)}, u32[]{:S(2)}) collective-permute-start(f32[4,64,512]{2,1,0:T(8,128)S(1)} %slice.579), channel_id=1, source_target_pairs={{1,0},{2,1},{3,2},{4,3},{5,4},{6,5},{7,6},{8,7},{9,8},{10,9},{11,1... | collective-permute-start | bytes 1572872 | tf_op jit(solution)/shard_map/ppermute | solution.py:28
  247.3 9.8 %multiply_bitcast_fusion = f32[4,16,16,512]{3,2,0,1:T(8,128)} fusion(f32[16,4,16,512]{3,2,1,0:T(8,128)} %reshape.635, f32[16,4,16,512]{3,2,1,0:T(8,128)} %mul.427, f32[16,4,16,512]{3,2,1,0:T(8,128)} %mul.383, f32[16,4,16,512]{3,2,1,0:T(8,128)} %mul.405, f32[16,4,16,512]{3,2,1,0:T(8,128)} %reshape.632, f32[16,4,16,512]{3,2,1,0:T(8,128)} %mul.358, ...), kind=kLoop, calls=%fused_computation.263 | loop fusion | flops 13107200 | bytes 23074816 | tf_op jit(solution)/shard_map/transpose | solution.py:36
  257.1 1.5 reshape.636
  258.6 1.5 broadcast_in_dim_reshape.7
  260.1 3.2 %copy.67 = f32[4,16,16,512]{3,2,1,0:T(8,128)} copy(f32[4,16,16,512]{3,2,0,1:T(8,128)} %multiply_bitcast_fusion) | data formatting | bytes 4194304 | tf_op jit(solution)/shard_map/transpose | solution.py:36
  263.3 4.6 %all-to-all-start = ((f32[4,16,16,512]{3,2,1,0:T(8,128)}), f32[4,16,16,512]{3,2,1,0:T(8,128)}, u32[]{:S(2)}, u32[]{:S(2)}) async-start(f32[4,16,16,512]{3,2,1,0:T(8,128)} %copy.67), calls=%async_computation | async-start | bytes 4194304 | tf_op jit(solution)/shard_map/all_to_all | solution.py:41
  267.9 1.1 constant_dynamic-update-slice_fusion.11
  271.2 4.9 %fusion.114 = f32[16,64,512]{2,1,0:T(8,128)S(1)} fusion(f32[16,64,512]{2,1,0:T(8,128)S(1)} %copy-done.7, f32[16,64,512]{2,1,0:T(8,128)S(1)} %copy-done.11, f32[20,64,512]{2,1,0:T(8,128)S(1)} %get-tuple-element.48, f32[20,64,512]{2,1,0:T(8,128)S(1)} %constant_dynamic-update-slice_fusion.8, f32[16,64,512]{2,1,0:T(8,128)S(1)} %copy-done.1), kind=kLoop, calls=%fused_computation.198 | loop fusion | flops 21495808 | bytes 25165824 | tf_op jit(solution)/shard_map/add | solution.py:110
  276.6 2.7 scatter_fusion.3
  279.3 1.5 broadcast_in_dim_reshape.6
  280.8 12.8 %all-to-all-done = f32[4,16,16,512]{3,2,1,0:T(8,128)} async-done(((f32[4,16,16,512]{3,2,1,0:T(8,128)}), f32[4,16,16,512]{3,2,1,0:T(8,128)}, u32[]{:S(2)}, u32[]{:S(2)}) %all-to-all-start) | async-done | bytes 2097184 | tf_op jit(solution)/shard_map/all_to_all | solution.py:41
  293.6 2.7 reduce_sum.105
  (90 shorter events, 14.1 us)
Async XLA Ops:
  2.9 59.2 %collective-permute-start.1 = (f32[4,64,512]{2,1,0:T(8,128)}, f32[4,64,512]{2,1,0:T(8,128)}, u32[]{:S(2)}, u32[]{:S(2)}) collective-permute-start(f32[4,64,512]{2,1,0:T(8,128)} %get-tuple-element.58), channel_id=1, source_target_pairs={{0,1},{1,2},{2,3},{3,4},{4,5},{5,6},{6,7},{7,8},{8,9},{9,10},{10,1... | collective-permute-start | bytes 1572872 | tf_op jit(solution)/shard_map/ppermute | solution.py:25
  8.0 54.1 %collective-permute-start = (f32[4,64,512]{2,1,0:T(8,128)}, f32[4,64,512]{2,1,0:T(8,128)}, u32[]{:S(2)}, u32[]{:S(2)}) collective-permute-start(f32[4,64,512]{2,1,0:T(8,128)} %get-tuple-element.57), channel_id=1, source_target_pairs={{1,0},{2,1},{3,2},{4,3},{5,4},{6,5},{7,6},{8,7},{9,8},{10,9},{11,1... | collective-permute-start | bytes 1572872 | tf_op jit(solution)/shard_map/ppermute | solution.py:28
  15.2 5.1 %copy-start.16 = (s32[1,6,16,64,128]{4,3,2,1,0:T(8,128)S(1)}, s32[1,6,16,64,128]{4,3,2,1,0:T(8,128)}, u32[]{:S(2)}) copy-start(s32[1,6,16,64,128]{4,3,2,1,0:T(8,128)} %param.14) | copy-start | bytes 9437188
  20.4 1.6 copy-start.17
  20.4 1.6 copy-start.21
  28.5 1.4 copy-start.20
  29.9 13.9 %copy-start.12 = (f32[16,64,4,128]{3,2,1,0:T(4,128)}, f32[16,64,4,128]{3,2,1,0:T(4,128)S(1)}, u32[]{:S(2)}) copy-start(f32[16,64,4,128]{3,2,1,0:T(4,128)S(1)} %copy.62) | copy-start | bytes 6291460
  51.7 1.7 copy-start.15
  53.5 8.0 %copy-start.19 = (f32[1,4,256]{2,1,0:T(4,128)S(1)}, f32[1,4,256]{2,1,0:T(4,128)}, u32[]{:S(2)}) copy-start(f32[1,4,256]{2,1,0:T(4,128)} %param.18) | copy-start | bytes 12292
  53.5 8.7 %copy-start.4 = (f32[16,64,512]{2,1,0:T(8,128)S(1)}, f32[16,64,512]{2,1,0:T(8,128)}, u32[]{:S(2)}) copy-start(f32[16,64,512]{2,1,0:T(8,128)} %param.13) | copy-start | bytes 6291460
  94.1 3.2 %copy-start.8 = (f32[524288]{0:T(1024)}, f32[524288]{0:T(1024)S(1)}, u32[]{:S(2)}) copy-start(f32[524288]{0:T(1024)S(1)} %scatter_fusion) | copy-start | bytes 6291460
  95.3 86.9 %collective-permute-start.3 = (f32[4,64,512]{2,1,0:T(8,128)}, f32[4,64,512]{2,1,0:T(8,128)}, u32[]{:S(2)}, u32[]{:S(2)}) collective-permute-start(f32[4,64,512]{2,1,0:T(8,128)} %slice.517), channel_id=1, source_target_pairs={{0,1},{1,2},{2,3},{3,4},{4,5},{5,6},{6,7},{7,8},{8,9},{9,10},{10,1... | collective-permute-start | bytes 1572872 | tf_op jit(solution)/shard_map/ppermute | solution.py:25
  97.3 87.0 %collective-permute-start.2 = (f32[4,64,512]{2,1,0:T(8,128)S(1)}, f32[4,64,512]{2,1,0:T(8,128)S(1)}, u32[]{:S(2)}, u32[]{:S(2)}) collective-permute-start(f32[4,64,512]{2,1,0:T(8,128)S(1)} %slice.514), channel_id=1, source_target_pairs={{1,0},{2,1},{3,2},{4,3},{5,4},{6,5},{7,6},{8,7},{9,8},{10,9},{11,1... | collective-permute-start | bytes 1572872 | tf_op jit(solution)/shard_map/ppermute | solution.py:28
  159.3 3.2 %copy-start.13 = (f32[16,64,4,128]{3,2,1,0:T(4,128)S(1)}, f32[16,64,4,128]{3,2,1,0:T(4,128)}, u32[]{:S(2)}) copy-start(f32[16,64,4,128]{3,2,1,0:T(4,128)} %copy-done.12) | copy-start | bytes 6291460
  164.4 3.2 %copy-start.14 = (f32[16,64,4,128]{3,2,1,0:T(4,128)S(1)}, f32[16,64,4,128]{3,2,1,0:T(4,128)}, u32[]{:S(2)}) copy-start(f32[16,64,4,128]{3,2,1,0:T(4,128)} %copy.51) | copy-start | bytes 6291460
  177.3 2.5 copy-start.18
  182.2 2.1 copy-start.2
  183.7 1.6 copy-start.5
  183.7 2.2 copy-start.10
  197.5 16.0 %copy-start.9 = (f32[524288]{0:T(1024)S(1)}, f32[524288]{0:T(1024)}, u32[]{:S(2)}) copy-start(f32[524288]{0:T(1024)} %copy-done.8) | copy-start | bytes 6291460
  199.8 22.5 %collective-permute-start.5 = (f32[4,64,512]{2,1,0:T(8,128)}, f32[4,64,512]{2,1,0:T(8,128)S(1)}, u32[]{:S(2)}, u32[]{:S(2)}) collective-permute-start(f32[4,64,512]{2,1,0:T(8,128)} %slice.548), channel_id=1, source_target_pairs={{0,1},{1,2},{2,3},{3,4},{4,5},{5,6},{6,7},{7,8},{8,9},{9,10},{10,1... | collective-permute-start | bytes 1572872 | tf_op jit(solution)/shard_map/ppermute | solution.py:25
  208.3 17.0 %collective-permute-start.4 = (f32[4,64,512]{2,1,0:T(8,128)}, f32[4,64,512]{2,1,0:T(8,128)S(1)}, u32[]{:S(2)}, u32[]{:S(2)}) collective-permute-start(f32[4,64,512]{2,1,0:T(8,128)} %slice.545), channel_id=1, source_target_pairs={{1,0},{2,1},{3,2},{4,3},{5,4},{6,5},{7,6},{8,7},{9,8},{10,9},{11,1... | collective-permute-start | bytes 1572872 | tf_op jit(solution)/shard_map/ppermute | solution.py:28
  216.8 8.6 %copy-start = (f32[16,64,512]{2,1,0:T(8,128)}, f32[16,64,512]{2,1,0:T(8,128)S(1)}, u32[]{:S(2)}) copy-start(f32[16,64,512]{2,1,0:T(8,128)S(1)} %reshape.633) | copy-start | bytes 6291460
  222.3 3.1 %copy-start.3 = (f32[16,64,512]{2,1,0:T(8,128)S(1)}, f32[16,64,512]{2,1,0:T(8,128)}, u32[]{:S(2)}) copy-start(f32[16,64,512]{2,1,0:T(8,128)} %copy-done.2) | copy-start | bytes 6291460
  222.4 3.1 %copy-start.6 = (f32[16,64,512]{2,1,0:T(8,128)S(1)}, f32[16,64,512]{2,1,0:T(8,128)}, u32[]{:S(2)}) copy-start(f32[16,64,512]{2,1,0:T(8,128)} %param.13) | copy-start | bytes 6291460
  236.0 31.9 %collective-permute-start.7 = (f32[4,64,512]{2,1,0:T(8,128)}, f32[4,64,512]{2,1,0:T(8,128)}, u32[]{:S(2)}, u32[]{:S(2)}) collective-permute-start(f32[4,64,512]{2,1,0:T(8,128)} %slice.582), channel_id=1, source_target_pairs={{0,1},{1,2},{2,3},{3,4},{4,5},{5,6},{6,7},{7,8},{8,9},{9,10},{10,1... | collective-permute-start | bytes 1572872 | tf_op jit(solution)/shard_map/ppermute | solution.py:25
  241.0 28.5 %collective-permute-start.6 = (f32[4,64,512]{2,1,0:T(8,128)S(1)}, f32[4,64,512]{2,1,0:T(8,128)S(1)}, u32[]{:S(2)}, u32[]{:S(2)}) collective-permute-start(f32[4,64,512]{2,1,0:T(8,128)S(1)} %slice.579), channel_id=1, source_target_pairs={{1,0},{2,1},{3,2},{4,3},{5,4},{6,5},{7,6},{8,7},{9,8},{10,9},{11,1... | collective-permute-start | bytes 1572872 | tf_op jit(solution)/shard_map/ppermute | solution.py:28
  263.3 5.7 %copy-start.11 = (f32[16,64,512]{2,1,0:T(8,128)S(1)}, f32[16,64,512]{2,1,0:T(8,128)}, u32[]{:S(2)}) copy-start(f32[16,64,512]{2,1,0:T(8,128)} %reshape.636) | copy-start | bytes 6291460
  263.3 30.3 %all-to-all-start = ((f32[4,16,16,512]{3,2,1,0:T(8,128)}), f32[4,16,16,512]{3,2,1,0:T(8,128)}, u32[]{:S(2)}, u32[]{:S(2)}) async-start(f32[4,16,16,512]{3,2,1,0:T(8,128)} %copy.67), calls=%async_computation | async-start | bytes 4194304 | tf_op jit(solution)/shard_map/all_to_all | solution.py:41
  269.0 1.6 copy-start.1
  269.0 2.2 copy-start.7
where the time goes:
time: 302 us; the launch traced here: 298 us
  other arithmetic  94.5 us (31%)
  local copies, waits for them, and re-layouts  79.8 us (26%)
  blocking collectives  51 us (17%)
  starting transfers between devices  49.2 us (16%)
  waiting for transfers between devices  17.2 us (6%)
  between operations  6.05 us (2%)
    psum x5, blocking collectives, by_axis(): return functools.reduce(lax.psum, axes, x)  51 us
    add x4, other arithmetic, body(): stepped = 2.0 * now - later + courant * laplace(now)  43 us
    mul x18, local copies, waits for them, and re-layouts, decode(): centred.reshape(depth, rows, cols // QBLOCK, QBLOCK)  31.9 us
    ppermute x4, starting transfers between devices, with_halo(): lax.ppermute(lax.slice_in_dim(block, 0, width, axis=dim), axis, backward)  27 us
    ppermute x4, starting transfers between devices, with_halo(): lax.ppermute(lax.slice_in_dim(block, block.shape[dim] - width, None, axis...  17.6 us
    mul x3, other arithmetic, decode(): centred.reshape(depth, rows, cols // QBLOCK, QBLOCK)  15 us
    scatter-add x4, other arithmetic, body(): stepped.reshape(-1).at[cells].add(residual).reshape(depth, rows, cols)  13.2 us
    all_to_all x1, waiting for transfers between devices, sum_at_owner(): lax.all_to_all(tiles, axis, split_axis=0, concat_axis=0, tiled=True)  12.8 us
  transfers between devices with their start and end apart: 9, of which 3 were waited for; matrix products, arithmetic and copies ran while one was open for 36% of the time, Pallas kernels for 0%

commit v1 on v0

v1 whole, which is shorter than its diff:
```python
import functools

import jax
import jax.numpy as jnp
from jax import lax
from jax.experimental import pallas as pl
from jax.experimental.pallas import tpu as pltpu
from jax.sharding import PartitionSpec as P

STEPS = 4
MUTE = 8
RADIUS = 4
LANES = 128
PAD = 8
CHUNKS = 4
COEFFS = (-205.0 / 72.0, 8.0 / 5.0, -1.0 / 5.0, 8.0 / 315.0, -1.0 / 560.0)
MESH = pl.DeviceIdType.MESH


def kernel(
    space_size,
    shot_size,
    table,
    source,
    now_hbm,
    later_hbm,
    courant_hbm,
    codes_hbm,
    index_hbm,
    cells_hbm,
    observed_hbm,
    grad_hbm,
    first_hbm,
    second_hbm,
    misfit_hbm,
    field,
    courant,
    words,
    index,
    cells,
    observed,
    scales,
    flipped,
    spread,
    rows_hot,
    cols_hot,
    values,
    injected,
    image,
    from_sibling,
    combined,
    from_partner,
    grad_out,
    sums,
    sums_in,
    load_sem,
    out_sem,
    halo_send,
    halo_recv,
    image_send,
    image_recv,
    sum_send,
    sum_recv,
):
    depth = courant.shape[1]
    height = courant.shape[2]
    tall = height // CHUNKS
    receivers = cells.shape[1]
    me = lax.axis_index("space")
    shot = lax.axis_index("shot")
    side, core = shot // 2, shot % 2
    up, down = (me + 1) % space_size, (me + space_size - 1) % space_size
    sibling = shot + 1 - 2 * core
    partner = (shot + 2) % 4

    loads = []

    def load(src, dst):
        copy = pltpu.make_async_copy(src, dst, load_sem.at[len(loads)])
        copy.start()
        loads.append(copy)
        return copy

    def lanes(xc):
        return pl.ds(xc * LANES, LANES)

    edges = []
    for xc in range(4):
        for z in (0, depth - RADIUS):
            edges.append(
                load(
                    now_hbm.at[0, pl.ds(z, RADIUS), :, lanes(xc)],
                    field.at[1, xc, pl.ds(RADIUS + z, RADIUS), pl.ds(PAD, height), :],
                )
            )
    small = [
        load(index_hbm.at[0], index),
        load(cells_hbm, cells),
        load(observed_hbm.at[0], observed),
    ]
    small_words = load(codes_hbm.at[0], words)
    rest = []
    for xc in range(4):
        rest.append(
            load(
                now_hbm.at[0, pl.ds(RADIUS, depth - 2 * RADIUS), :, lanes(xc)],
                field.at[1, xc, pl.ds(2 * RADIUS, depth - 2 * RADIUS), pl.ds(PAD, height), :],
            )
        )
        rest.append(
            load(
                later_hbm.at[0, :, :, lanes(xc)],
                field.at[0, xc, pl.ds(RADIUS, depth), pl.ds(PAD, height), :],
            )
        )
        rest.append(load(courant_hbm.at[:, :, lanes(xc)], courant.at[xc]))

    def flip(i, bit):
        return i + bit - 2 * bit * ((i // bit) % 2)

    stages = []
    bit = 1
    while bit < space_size:
        stages.append({"space": flip(me, bit)})
        bit *= 2
    bit = 1
    while bit < shot_size:
        stages.append({"shot": flip(shot, bit)})
        bit *= 2
    peers = stages + [{"space": up}, {"space": down}]
    barrier = pltpu.get_barrier_semaphore()
    for peer in peers:
        pl.semaphore_signal(barrier, inc=1, device_id=peer, device_id_type=MESH)

    zero_rows = jnp.zeros((4, 1, PAD, LANES), jnp.float32)

    def clear_rows(i, carry):
        level = 1 + i // depth
        z = RADIUS + i % depth
        field[pl.ds(level, 1), :, pl.ds(z, 1), pl.ds(0, PAD), :] = zero_rows[None]
        field[pl.ds(level, 1), :, pl.ds(z, 1), pl.ds(PAD + height, PAD), :] = zero_rows[None]
        return carry

    lax.fori_loop(0, STEPS * depth, clear_rows, 0)
    zero_plane = jnp.zeros((1, 4, 1, height, LANES), jnp.float32)

    @pl.when(me == 0)
    def _():
        def clear(i, carry):
            field[pl.ds(1 + i // RADIUS, 1), :, pl.ds(i % RADIUS, 1), pl.ds(PAD, height), :] = (
                zero_plane
            )
            return carry

        lax.fori_loop(0, STEPS * RADIUS, clear, 0)

    @pl.when(me == space_size - 1)
    def _():
        def clear(i, carry):
            field[
                pl.ds(1 + i // RADIUS, 1),
                :,
                pl.ds(RADIUS + depth + i % RADIUS, 1),
                pl.ds(PAD, height),
                :,
            ] = zero_plane
            return carry

        lax.fori_loop(0, STEPS * RADIUS, clear, 0)

    pl.semaphore_wait(barrier, len(peers))

    def rows_of(n):
        c = (n + 2 * (1 - side)) % CHUNKS
        return c, pl.multiple_of(PAD + c * tall, 8)

    def halo_copy(t, n, way):
        _, row = rows_of(n)
        src_z, dst_z, target = ((depth, 0, up), (RADIUS, RADIUS + depth, down))[way]
        return pltpu.make_async_remote_copy(
            src_ref=field.at[1 + t, :, pl.ds(src_z, RADIUS), pl.ds(row, tall), :],
            dst_ref=field.at[1 + t, :, pl.ds(dst_z, RADIUS), pl.ds(row, tall), :],
            send_sem=halo_send.at[way, t, n],
            recv_sem=halo_recv.at[way, t, n],
            device_id={"space": target},
            device_id_type=MESH,
        )

    has_up = me < space_size - 1
    has_down = me > 0

    def send_halo(t, n):
        @pl.when(has_up)
        def _():
            halo_copy(t, n, 0).start()

        @pl.when(has_down)
        def _():
            halo_copy(t, n, 1).start()

    def wait_halo(t, n):
        @pl.when(has_down)
        def _():
            halo_copy(t, n, 0).wait_recv()

        @pl.when(has_up)
        def _():
            halo_copy(t, n, 1).wait_recv()

    for copy in edges:
        copy.wait()

    def first_sends(n, carry):
        send_halo(0, n)
        return carry

    lax.fori_loop(0, CHUNKS, first_sends, 0)

    for copy in small:
        copy.wait()
    levels = index.shape[0]
    flat_index = index[...].reshape(levels * depth, index.shape[2])

    def look_up(k, acc):
        return jnp.where(flat_index == k, table[k], acc)

    looked = lax.fori_loop(0, table.shape[0], look_up, jnp.zeros(flat_index.shape, jnp.float32))
    scales[pl.ds(0, levels * depth), :] = looked
    scales[pl.ds(levels * depth, LANES - levels * depth), :] = jnp.zeros(
        (LANES - levels * depth, index.shape[2]), jnp.float32
    )
    flipped[...] = scales[...].T
    columns = [flipped[pl.ds(m, height, stride=4), :] for m in range(4)]

    def spread_one(i, carry):
        level, z = i // depth, i % depth
        for m in range(4):
            moved = pltpu.roll(columns[m], LANES - i, 1)
            spread[pl.ds(level, 1), pl.ds(z, 1), m, :, :] = jnp.broadcast_to(
                moved[:, 0:1], (height, LANES)
            )[None, None]
        return carry

    for m in range(4):
        spread[0, 0, m, :, :] = jnp.broadcast_to(columns[m][:, 0:1], (height, LANES))
    lax.fori_loop(1, levels * depth, spread_one, 0)

    width = 4 * LANES
    cell = cells[...] - me * (depth * height * width)
    row_of = cell // width
    col_of = cell % width
    block_of = (cell // LANES) % (4 * height)
    slab_of = row_of // height
    for z in range(depth):
        ids = z * height + lax.broadcasted_iota(jnp.int32, (height, receivers), 0)
        rows_hot[z] = jnp.where(ids == row_of, 1.0, 0.0).astype(jnp.bfloat16)
    col_ids = lax.broadcasted_iota(jnp.int32, (width, receivers), 0)
    cols_hot[...] = jnp.where(col_ids == col_of, 1.0, 0.0).astype(jnp.bfloat16)
    block_ids = lax.broadcasted_iota(jnp.int32, (4 * height, receivers), 0)
    blocks_hot = jnp.where(block_ids == block_of, 1.0, 0.0)
    scale_at = jnp.dot(
        scales[...], blocks_hot, precision=lax.Precision.HIGHEST, preferred_element_type=jnp.float32
    )
    depth_ids = lax.broadcasted_iota(jnp.int32, (depth, receivers), 0)
    small_words.wait()
    planes = 4
    total = jnp.zeros((1, receivers), jnp.float32)
    for t in range(STEPS):
        level = STEPS - t

        def gather(i, acc):
            w = words[level, pl.ds(i * planes, planes), :, :].reshape(planes * height, LANES)
            parts = [
                (((w >> (8 * m)) & 255) - 128).astype(jnp.float32).astype(jnp.bfloat16)
                for m in range(4)
            ]
            found = jnp.dot(
                jnp.concatenate(parts, axis=1), cols_hot[...], preferred_element_type=jnp.float32
            )
            hot = rows_hot[pl.ds(i * planes, planes), :, :].reshape(planes * height, receivers)
            return acc + jnp.sum(found * hot.astype(jnp.float32), axis=0, keepdims=True)

        code = lax.fori_loop(
            0, depth // planes, gather, jnp.zeros((1, receivers), jnp.float32)
        )
        part = scale_at[level * depth : (level + 1) * depth]
        scale = jnp.sum(jnp.where(depth_ids == slab_of, part, 0.0), axis=0, keepdims=True)
        residual = code * scale - observed[level - 1 : level, :]
        total = total + residual * residual
        left = residual
        for piece in range(3):
            short = left.astype(jnp.bfloat16).astype(jnp.float32)
            left = left - short
            values[t, piece] = jnp.where(col_ids == col_of, short, 0.0).astype(jnp.bfloat16)
    sums[0] = jnp.broadcast_to(
        jnp.sum(total, axis=1, keepdims=True), sums.shape[1:]
    )

    def sum_copy(b):
        return pltpu.make_async_remote_copy(
            src_ref=sums.at[b],
            dst_ref=sums_in.at[b],
            send_sem=sum_send.at[b],
            recv_sem=sum_recv.at[b],
            device_id=stages[b],
            device_id_type=MESH,
        )

    for copy in rest:
        copy.wait()

    lane = lax.broadcasted_iota(jnp.int32, (tall, LANES), 1)

    def update(t, c, row, z):
        def at(xc, dz, dy):
            return field[1 + t, xc, RADIUS + z + dz, pl.ds(row + dy, tall), :]

        centre = [at(xc, 0, 0) for xc in range(4)]
        after = [[pltpu.roll(v, LANES - i, 1) for v in centre] for i in range(1, 5)]
        before = [[pltpu.roll(v, i, 1) for v in centre] for i in range(1, 5)]
        for xc in range(4):
            acc = (3.0 * COEFFS[0]) * centre[xc]
            for i in range(1, 5):
                nxt = after[i - 1][xc + 1] if xc < 3 else 0.0
                prv = before[i - 1][xc - 1] if xc > 0 else 0.0
                pair = jnp.where(lane < LANES - i, after[i - 1][xc], nxt) + jnp.where(
                    lane >= i, before[i - 1][xc], prv
                )
                pair = pair + (at(xc, i, 0) + at(xc, -i, 0)) + (at(xc, 0, i) + at(xc, 0, -i))
                acc = acc + COEFFS[i] * pair
            y0 = pl.multiple_of(row - PAD, 8)
            old = field[t, xc, RADIUS + z, pl.ds(row, tall), :]
            new = 2.0 * centre[xc] - old + courant[xc, z, pl.ds(y0, tall), :] * acc
            field[2 + t, xc, RADIUS + z, pl.ds(row, tall), :] = new + injected[xc, z, :, :]

    def inject(t, c):
        hot = rows_hot[:, pl.ds(pl.multiple_of(c * tall, 16), tall), :].reshape(
            depth * tall, receivers
        )
        acc = None
        for piece in range(3):
            term = lax.dot_general(
                hot,
                values[t, piece],
                (((1,), (1,)), ((), ())),
                preferred_element_type=jnp.float32,
            )
            acc = term if acc is None else acc + term
        for xc in range(4):
            injected[xc] = acc[:, xc * LANES : (xc + 1) * LANES].reshape(depth, tall, LANES)

    def add_image(t, c, row, first):
        level = STEPS - t
        y0 = pl.multiple_of(row - PAD, 8)

        def plane(z, carry):
            ws = [words[level + d, z, pl.ds(y0, tall), :] for d in (-1, 0, 1)]
            for m in range(4):
                f = [
                    (((w >> (8 * m)) & 255) - 128).astype(jnp.float32)
                    * spread[level + d, z, m, pl.ds(y0, tall), :]
                    for w, d in zip(ws, (-1, 0, 1))
                ]
                term = field[1 + t, m, RADIUS + z, pl.ds(row, tall), :] * (
                    f[2] - 2.0 * f[1] + f[0]
                )
                if first:
                    image[c, m, z] = term
                else:
                    image[c, m, z] = image[c, m, z] + term
            return carry

        lax.fori_loop(0, depth, plane, 0)

    def mute(c):
        y = c * tall + lax.broadcasted_iota(jnp.int32, (tall, LANES), 0)
        across = [(y - source[1]) ** 2 + (m * LANES + lane - source[2]) ** 2 for m in range(4)]

        def plane(z, carry):
            dz = me * depth + z - source[0]
            for m in range(4):
                dist = (across[m] + dz * dz).astype(jnp.float32)
                image[c, m, z] = image[c, m, z] * (1.0 - jnp.exp(-dist / (2.0 * MUTE * MUTE)))
            return carry

        lax.fori_loop(0, depth, plane, 0)

    far = 2 * (1 - side) + core
    near = shot

    def pair_copy(c, slot):
        return pltpu.make_async_remote_copy(
            src_ref=image.at[c],
            dst_ref=from_sibling.at[slot],
            send_sem=image_send.at[slot],
            recv_sem=image_recv.at[slot],
            device_id={"shot": sibling},
            device_id_type=MESH,
        )

    sibling_far = 2 * (1 - side) + 1 - core
    far_copy = pair_copy(sibling_far, 0)
    near_copy = pair_copy(sibling, 1)
    partner_copy = pltpu.make_async_remote_copy(
        src_ref=combined,
        dst_ref=from_partner,
        send_sem=image_send.at[2],
        recv_sem=image_recv.at[2],
        device_id={"shot": partner},
        device_id_type=MESH,
    )

    outs = []

    def store(src, dst):
        copy = pltpu.make_async_copy(src, dst, out_sem.at[len(outs)])
        copy.start()
        outs.append(copy)

    def first_copy(n, xc):
        c, row = rows_of(n)
        return pltpu.make_async_copy(
            field.at[1 + STEPS, xc, pl.ds(RADIUS, depth), pl.ds(row, tall), :],
            first_hbm.at[0, :, pl.ds(pl.multiple_of(row - PAD, 8), tall), lanes(xc)],
            out_sem.at[16 + n * 4 + xc],
        )

    for t in range(STEPS):

        def task(n, carry, t=t):
            c, row = rows_of(n)
            if t < 2:
                for j in range(4):
                    b = 4 * t + j

                    @pl.when(n == j)
                    def _():
                        if b > 0:
                            sum_copy(b - 1).wait_recv()
                            sums[b] = sums[b - 1] + sums_in[b - 1]
                        sum_copy(b).start()

            inject(t, c)

            def inner(z, carry):
                update(t, c, row, z)
                return carry

            lax.fori_loop(RADIUS, depth - RADIUS, inner, 0)
            if t == 0:
                add_image(0, c, row, True)
            if t == 2:

                @pl.when(n == 2)
                def _():
                    far_copy.wait_recv()

                    def plane(z, carry):
                        for m in range(4):
                            combined[m, z] = image[far, m, z] + from_sibling[0, m, z]
                        return carry

                    lax.fori_loop(0, depth, plane, 0)
                    partner_copy.start()

            if t == 3:

                @pl.when(n == 3)
                def _():
                    near_copy.wait_recv()
                    partner_copy.wait_recv()

                    def plane(z, carry):
                        for m in range(4):
                            grad_out[m, z] = (
                                image[near, m, z] + from_sibling[1, m, z] + from_partner[m, z]
                            )
                        return carry

                    lax.fori_loop(0, depth, plane, 0)

            wait_halo(t, n)

            def outer(z, carry):
                update(t, c, row, z)
                update(t, c, row, depth - RADIUS + z)
                return carry

            lax.fori_loop(0, RADIUS, outer, 0)
            if t < STEPS - 1:
                send_halo(t + 1, n)
                add_image(t + 1, c, row, False)
            else:
                for xc in range(4):
                    first_copy(n, xc).start()
            if t == 2:
                mute(c)

                @pl.when(c == sibling_far)
                def _():
                    far_copy.start()

                @pl.when(c == sibling)
                def _():
                    near_copy.start()

            return carry

        lax.fori_loop(0, CHUNKS, task, 0)
        if t == 1:
            last = len(stages) - 1
            sum_copy(last).wait_recv()
            sums[last + 1] = sums[last] + sums_in[last]
        if t == 2:
            for xc in range(4):
                store(
                    field.at[STEPS, xc, pl.ds(RADIUS, depth), pl.ds(PAD, height), :],
                    second_hbm.at[0, :, :, lanes(xc)],
                )
            store(sums.at[len(stages)], misfit_hbm)
    for xc in range(4):
        store(grad_out.at[xc], grad_hbm.at[:, :, lanes(xc)])

    def drain(n, carry):
        for t in range(STEPS):

            @pl.when(has_up)
            def _():
                halo_copy(t, n, 0).wait_send()

            @pl.when(has_down)
            def _():
                halo_copy(t, n, 1).wait_send()

        for xc in range(4):
            first_copy(n, xc).wait()
        return carry

    far_copy.wait_send()
    near_copy.wait_send()
    partner_copy.wait_send()
    for b in range(len(stages)):
        sum_copy(b).wait_send()
    lax.fori_loop(0, CHUNKS, drain, 0)
    for copy in outs:
        copy.wait()


def body(
    space_size,
    shot_size,
    adjoint_now,
    adjoint_later,
    courant,
    checkpoint_codes,
    scale_index,
    scale_table,
    receiver_cell,
    observed,
    source_cell,
):
    _, depth, height, width = adjoint_now.shape
    levels = checkpoint_codes.shape[1]
    receivers = receiver_cell.shape[1]
    tall = height // CHUNKS
    quarter = (4, depth, tall, LANES)
    stages = (space_size * shot_size).bit_length() - 1
    whole = pl.BlockSpec(memory_space=pl.ANY)
    scalars = pl.BlockSpec(memory_space=pltpu.SMEM)
    f32 = jnp.float32
    gradient, first, second, misfit = pl.pallas_call(
        functools.partial(kernel, space_size, shot_size),
        out_shape=(
            jax.ShapeDtypeStruct((depth, tall, width), f32),
            jax.ShapeDtypeStruct(adjoint_now.shape, f32),
            jax.ShapeDtypeStruct(adjoint_now.shape, f32),
            jax.ShapeDtypeStruct((8, LANES), f32),
        ),
        in_specs=[scalars, scalars] + [whole] * 7,
        out_specs=[whole] * 4,
        scratch_shapes=[
            pltpu.VMEM((STEPS + 2, 4, depth + 2 * RADIUS, height + 2 * PAD, LANES), f32),
            pltpu.VMEM((4, depth, height, LANES), f32),
            pltpu.VMEM((levels, depth, height, LANES), jnp.int32),
            pltpu.VMEM((levels, depth, 4 * height), jnp.int32),
            pltpu.VMEM((1, receivers), jnp.int32),
            pltpu.VMEM((STEPS, receivers), f32),
            pltpu.VMEM((LANES, 4 * height), f32),
            pltpu.VMEM((4 * height, LANES), f32),
            pltpu.VMEM((levels, depth, 4, height, LANES), f32),
            pltpu.VMEM((depth, height, receivers), jnp.bfloat16),
            pltpu.VMEM((width, receivers), jnp.bfloat16),
            pltpu.VMEM((STEPS, 3, width, receivers), jnp.bfloat16),
            pltpu.VMEM(quarter, f32),
            pltpu.VMEM((CHUNKS, *quarter), f32),
            pltpu.VMEM((2, *quarter), f32),
            pltpu.VMEM(quarter, f32),
            pltpu.VMEM(quarter, f32),
            pltpu.VMEM(quarter, f32),
            pltpu.VMEM((stages + 1, 8, LANES), f32),
            pltpu.VMEM((stages, 8, LANES), f32),
            pltpu.SemaphoreType.DMA((32,)),
            pltpu.SemaphoreType.DMA((32,)),
            pltpu.SemaphoreType.DMA((2, STEPS, CHUNKS)),
            pltpu.SemaphoreType.DMA((2, STEPS, CHUNKS)),
            pltpu.SemaphoreType.DMA((3,)),
            pltpu.SemaphoreType.DMA((3,)),
            pltpu.SemaphoreType.DMA((stages,)),
            pltpu.SemaphoreType.DMA((stages,)),
        ],
        compiler_params=pltpu.CompilerParams(
            collective_id=0, has_side_effects=True, vmem_limit_bytes=60 * 1024 * 1024
        ),
    )(
        scale_table,
        source_cell[0],
        adjoint_now,
        adjoint_later,
        courant,
        checkpoint_codes,
        scale_index,
        receiver_cell,
        observed,
    )
    count = shot_size * STEPS * receivers * space_size
    return gradient, first, second, 0.5 * misfit[0, 0] / count


def solution(mesh):
    sizes = dict(mesh.shape)
    return jax.shard_map(
        functools.partial(body, sizes["space"], sizes["shot"]),
        mesh=mesh,
        in_specs=(
            P("shot", "space", None, None),
            P("shot", "space", None, None),
            P("space", None, None),
            P("shot", None, "space", None, None),
            P("shot", None, "space", None),
            P(),
            P("shot", "space"),
            P("shot", None, "space"),
            P("shot", None),
        ),
        out_specs=(
            P("space", "shot", None),
            P("shot", "space", None, None),
            P("shot", "space", None, None),
            P(),
        ),
        check_vma=False,
    )
```

time: 302 us -> 132 us (0.44); the launches traced: 298 us -> 131 us
  Pallas kernels: 0 us -> 121 us
  other arithmetic: 94.5 us -> 0 us
  local copies, waits for them, and re-layouts: 79.8 us -> 7.68 us
  blocking collectives: 51 us -> 0 us
  starting transfers between devices: 49.2 us -> 0 us
  waiting for transfers between devices: 17.2 us -> 0 us
  between operations: 6.05 us -> 2.43 us
    pallas_call x0 -> x1, Pallas kernels: none -> 121 us  [body(): pl.pallas_call(functools.partial(kernel, space_size, shot_size), out_shap...]
    psum x5 -> x0, blocking collectives: 51 us -> none  [by_axis(): return functools.reduce(lax.psum, axes, x)]
    ppermute x8 -> x0, starting transfers between devices: 44.6 us -> none  [the longest x4 27 us: with_halo(): lax.ppermute(lax.slice_in_dim(block, 0, width, axis=dim), axis, backward)]
    add x5 -> x0, other arithmetic: 43.1 us -> none  [the longest x4 43 us: body(): stepped = 2.0 * now - later + courant * laplace(now)]
    mul x18 -> x0, local copies, waits for them, and re-layouts: 31.9 us -> none  [decode(): centred.reshape(depth, rows, cols // QBLOCK, QBLOCK)]
    mul x3 -> x0, other arithmetic: 15 us -> none  [decode(): centred.reshape(depth, rows, cols // QBLOCK, QBLOCK)]
    scatter-add x4 -> x0, other arithmetic: 13.2 us -> none  [body(): stepped.reshape(-1).at[cells].add(residual).reshape(depth, rows, cols)]
    all_to_all x1 -> x0, waiting for transfers between devices: 12.8 us -> none  [sum_at_owner(): lax.all_to_all(tiles, axis, split_axis=0, concat_axis=0, tiled=True)]
  transfers between devices with their start and end apart: 9 -> 0, of which waited for: 3 -> 0; matrix products, arithmetic and copies ran while one was open for 36% -> 0% of each run, Pallas kernels for 0% -> 0%
where the time goes in v1:
time: 132 us; the launch traced here: 131 us
  Pallas kernels  121 us (92%)
  local copies, waits for them, and re-layouts  7.68 us (6%)
  between operations  2.43 us (2%)
    pallas_call x1, Pallas kernels, body(): pl.pallas_call(functools.partial(kernel, space_size, shot_size), out_shap...  121 us
    unnamed x5, local copies, waits for them, and re-layouts  6.5 us

profile of v1, /device:TPU:2, one launch (start us, length us, event | category | flops | bytes accessed | tf_op | source)
XLA Modules:
  0.0 131.3 jit_solution(7149247581569767588)
XLA Ops:
  0.6 121.2 %shard_map.120 = (f32[16,16,512]{2,1,0:T(8,128)}, f32[1,16,64,512]{3,2,1,0:T(8,128)}, f32[1,16,64,512]{3,2,1,0:T(8,128)}, f32[8,128]{1,0:T(8,128)}) custom-call(f32[64]{0:T(128)} %table.1, s32[3]{0:T(128)} %bitcast.2, f32[1,16,64,512]{3,2,1,0:T(8,128)} %now_hbm.1, f32[1,16,64,512]{3,2,1,0:T(8,128)} %later_hbm.1, f32[16,64,512]{2,1,0:T(8,128)} %courant_hbm.1, ...), custom_call_target="tpu_custom_call" | custom-call | tf_op jit(solution)/shard_map/pallas_call | solution.py:571
  121.9 1.2 slice.3
  123.7 1.9 %copy.16 = f32[16,16,512]{2,1,0:T(8,128)} copy(f32[16,16,512]{2,1,0:T(8,128)} %get-tuple-element.16) | data formatting | bytes 1048576
  125.6 0.0 copy-start
  125.6 3.3 %copy.17 = f32[1,16,64,512]{3,2,1,0:T(8,128)} copy(f32[1,16,64,512]{3,2,1,0:T(8,128)} %get-tuple-element.17) | data formatting | bytes 4194304
  128.9 0.0 copy-done
  128.9 1.3 %copy.18 = f32[1,16,64,512]{3,2,1,0:T(8,128)} copy(f32[1,16,64,512]{3,2,1,0:T(8,128)S(1)} %copy-done) | data formatting | bytes 4194304
Async XLA Ops:
  125.6 3.3 %copy-start = (f32[1,16,64,512]{3,2,1,0:T(8,128)S(1)}, f32[1,16,64,512]{3,2,1,0:T(8,128)}, u32[]{:S(2)}) copy-start(f32[1,16,64,512]{3,2,1,0:T(8,128)} %get-tuple-element.18) | copy-start | bytes 6291460

commit v2 on v1

--- a/solution.py
+++ b/solution.py
@@ -20,8 +20,6 @@
 def kernel(
     space_size,
     shot_size,
-    table,
-    source,
     now_hbm,
     later_hbm,
     courant_hbm,
@@ -29,10 +27,14 @@
     index_hbm,
     cells_hbm,
     observed_hbm,
+    table_hbm,
+    source_hbm,
     grad_hbm,
     first_hbm,
     second_hbm,
     misfit_hbm,
+    table,
+    source_ref,
     field,
     courant,
     words,
@@ -62,6 +64,7 @@
     sum_send,
     sum_recv,
 ):
+    scale = 0.5 / (shot_size * STEPS * cells.shape[1] * space_size)
     depth = courant.shape[1]
     height = courant.shape[2]
     tall = height // CHUNKS
@@ -72,48 +75,6 @@
     up, down = (me + 1) % space_size, (me + space_size - 1) % space_size
     sibling = shot + 1 - 2 * core
     partner = (shot + 2) % 4
-
-    loads = []
-
-    def load(src, dst):
-        copy = pltpu.make_async_copy(src, dst, load_sem.at[len(loads)])
-        copy.start()
-        loads.append(copy)
-        return copy
-
-    def lanes(xc):
-        return pl.ds(xc * LANES, LANES)
-
-    edges = []
-    for xc in range(4):
-        for z in (0, depth - RADIUS):
-            edges.append(
-                load(
-                    now_hbm.at[0, pl.ds(z, RADIUS), :, lanes(xc)],
-                    field.at[1, xc, pl.ds(RADIUS + z, RADIUS), pl.ds(PAD, height), :],
-                )
-            )
-    small = [
-        load(index_hbm.at[0], index),
-        load(cells_hbm, cells),
-        load(observed_hbm.at[0], observed),
-    ]
-    small_words = load(codes_hbm.at[0], words)
-    rest = []
-    for xc in range(4):
-        rest.append(
-            load(
-                now_hbm.at[0, pl.ds(RADIUS, depth - 2 * RADIUS), :, lanes(xc)],
-                field.at[1, xc, pl.ds(2 * RADIUS, depth - 2 * RADIUS), pl.ds(PAD, height), :],
-            )
-        )
-        rest.append(
-            load(
-                later_hbm.at[0, :, :, lanes(xc)],
-                field.at[0, xc, pl.ds(RADIUS, depth), pl.ds(PAD, height), :],
-            )
-        )
-        rest.append(load(courant_hbm.at[:, :, lanes(xc)], courant.at[xc]))
 
     def flip(i, bit):
         return i + bit - 2 * bit * ((i // bit) % 2)
@@ -132,6 +93,89 @@
     for peer in peers:
         pl.semaphore_signal(barrier, inc=1, device_id=peer, device_id_type=MESH)
 
+    loads = []
+
+    def load(src, dst):
+        copy = pltpu.make_async_copy(src, dst, load_sem.at[len(loads)])
+        copy.start()
+        loads.append(copy)
+        return copy
+
+    def lanes(xc):
+        return pl.ds(xc * LANES, LANES)
+
+    edges = []
+    for xc in range(4):
+        for z in (0, depth - RADIUS):
+            edges.append(
+                load(
+                    now_hbm.at[0, pl.ds(z, RADIUS), :, lanes(xc)],
+                    field.at[1, xc, pl.ds(RADIUS + z, RADIUS), pl.ds(PAD, height), :],
+                )
+            )
+    small = [
+        load(index_hbm.at[0], index),
+        load(cells_hbm, cells),
+        load(observed_hbm.at[0], observed),
+        load(table_hbm, table),
+        load(source_hbm, source_ref),
+    ]
+    small_words = load(codes_hbm.at[0], words)
+    rest = []
+    for xc in range(4):
+        rest.append(
+            load(
+                now_hbm.at[0, pl.ds(RADIUS, depth - 2 * RADIUS), :, lanes(xc)],
+                field.at[1, xc, pl.ds(2 * RADIUS, depth - 2 * RADIUS), pl.ds(PAD, height), :],
+            )
+        )
+        rest.append(
+            load(
+                later_hbm.at[0, :, :, lanes(xc)],
+                field.at[0, xc, pl.ds(RADIUS, depth), pl.ds(PAD, height), :],
+            )
+        )
+        rest.append(load(courant_hbm.at[:, :, lanes(xc)], courant.at[xc]))
+
+    pl.semaphore_wait(barrier, len(peers))
+
+    def rows_of(n):
+        c = (n + 2 * (1 - side)) % CHUNKS
+        return c, pl.multiple_of(PAD + c * tall, 8)
+
+    def halo_copy(t, n, way):
+        _, row = rows_of(n)
+        src_z, dst_z, target = ((depth, 0, up), (RADIUS, RADIUS + depth, down))[way]
+        return pltpu.make_async_remote_copy(
+            src_ref=field.at[1 + t, :, pl.ds(src_z, RADIUS), pl.ds(row, tall), :],
+            dst_ref=field.at[1 + t, :, pl.ds(dst_z, RADIUS), pl.ds(row, tall), :],
+            send_sem=halo_send.at[way, t, n],
+            recv_sem=halo_recv.at[way, t, n],
+            device_id={"space": target},
+            device_id_type=MESH,
+        )
+
+    has_up = me < space_size - 1
+    has_down = me > 0
+
+    def send_halo(t, n):
+        @pl.when(has_up)
+        def _():
+            halo_copy(t, n, 0).start()
+
+        @pl.when(has_down)
+        def _():
+            halo_copy(t, n, 1).start()
+
+    for copy in edges:
+        copy.wait()
+
+    def first_sends(n, carry):
+        send_halo(0, n)
+        return carry
+
+    lax.fori_loop(0, CHUNKS, first_sends, 0)
+
     zero_rows = jnp.zeros((4, 1, PAD, LANES), jnp.float32)
 
     def clear_rows(i, carry):
@@ -168,56 +212,9 @@
 
         lax.fori_loop(0, STEPS * RADIUS, clear, 0)
 
-    pl.semaphore_wait(barrier, len(peers))
-
-    def rows_of(n):
-        c = (n + 2 * (1 - side)) % CHUNKS
-        return c, pl.multiple_of(PAD + c * tall, 8)
-
-    def halo_copy(t, n, way):
-        _, row = rows_of(n)
-        src_z, dst_z, target = ((depth, 0, up), (RADIUS, RADIUS + depth, down))[way]
-        return pltpu.make_async_remote_copy(
-            src_ref=field.at[1 + t, :, pl.ds(src_z, RADIUS), pl.ds(row, tall), :],
-            dst_ref=field.at[1 + t, :, pl.ds(dst_z, RADIUS), pl.ds(row, tall), :],
-            send_sem=halo_send.at[way, t, n],
-            recv_sem=halo_recv.at[way, t, n],
-            device_id={"space": target},
-            device_id_type=MESH,
-        )
-
-    has_up = me < space_size - 1
-    has_down = me > 0
-
-    def send_halo(t, n):
-        @pl.when(has_up)
-        def _():
-            halo_copy(t, n, 0).start()
-
-        @pl.when(has_down)
-        def _():
-            halo_copy(t, n, 1).start()
-
-    def wait_halo(t, n):
-        @pl.when(has_down)
-        def _():
-            halo_copy(t, n, 0).wait_recv()
-
-        @pl.when(has_up)
-        def _():
-            halo_copy(t, n, 1).wait_recv()
-
-    for copy in edges:
-        copy.wait()
-
-    def first_sends(n, carry):
-        send_halo(0, n)
-        return carry
-
-    lax.fori_loop(0, CHUNKS, first_sends, 0)
-
     for copy in small:
         copy.wait()
+    source = [source_ref[0, i] for i in range(3)]
     levels = index.shape[0]
     flat_index = index[...].reshape(levels * depth, index.shape[2])
 
@@ -230,21 +227,6 @@
         (LANES - levels * depth, index.shape[2]), jnp.float32
     )
     flipped[...] = scales[...].T
-    columns = [flipped[pl.ds(m, height, stride=4), :] for m in range(4)]
-
-    def spread_one(i, carry):
-        level, z = i // depth, i % depth
-        for m in range(4):
-            moved = pltpu.roll(columns[m], LANES - i, 1)
-            spread[pl.ds(level, 1), pl.ds(z, 1), m, :, :] = jnp.broadcast_to(
-                moved[:, 0:1], (height, LANES)
-            )[None, None]
-        return carry
-
-    for m in range(4):
-        spread[0, 0, m, :, :] = jnp.broadcast_to(columns[m][:, 0:1], (height, LANES))
-    lax.fori_loop(1, levels * depth, spread_one, 0)
-
     width = 4 * LANES
     cell = cells[...] - me * (depth * height * width)
     row_of = cell // width
@@ -284,8 +266,8 @@
             0, depth // planes, gather, jnp.zeros((1, receivers), jnp.float32)
         )
         part = scale_at[level * depth : (level + 1) * depth]
-        scale = jnp.sum(jnp.where(depth_ids == slab_of, part, 0.0), axis=0, keepdims=True)
-        residual = code * scale - observed[level - 1 : level, :]
+        factor = jnp.sum(jnp.where(depth_ids == slab_of, part, 0.0), axis=0, keepdims=True)
+        residual = code * factor - observed[level - 1 : level, :]
         total = total + residual * residual
         left = residual
         for piece in range(3):
@@ -331,7 +313,9 @@
             y0 = pl.multiple_of(row - PAD, 8)
             old = field[t, xc, RADIUS + z, pl.ds(row, tall), :]
             new = 2.0 * centre[xc] - old + courant[xc, z, pl.ds(y0, tall), :] * acc
-            field[2 + t, xc, RADIUS + z, pl.ds(row, tall), :] = new + injected[xc, z, :, :]
+            field[(2 + t) % (STEPS + 1), xc, RADIUS + z, pl.ds(row, tall), :] = (
+                new + injected[xc, z, :, :]
+            )
 
     def inject(t, c):
         hot = rows_hot[:, pl.ds(pl.multiple_of(c * tall, 16), tall), :].reshape(
@@ -348,6 +332,18 @@
             acc = term if acc is None else acc + term
         for xc in range(4):
             injected[xc] = acc[:, xc * LANES : (xc + 1) * LANES].reshape(depth, tall, LANES)
+
+    def spread_rows(c):
+        row = pl.multiple_of(c * tall, 8)
+        columns = [
+            flipped[pl.ds(pl.multiple_of(4 * c * tall, 8) + m, tall, stride=4), :]
+            for m in range(4)
+        ]
+        for i in range(levels * depth):
+            for m in range(4):
+                spread[i // depth, i % depth, m, pl.ds(row, tall), :] = jnp.broadcast_to(
+                    columns[m][:, i : i + 1], (tall, LANES)
+                )
 
     def add_image(t, c, row, first):
         level = STEPS - t
@@ -420,7 +416,7 @@
     def first_copy(n, xc):
         c, row = rows_of(n)
         return pltpu.make_async_copy(
-            field.at[1 + STEPS, xc, pl.ds(RADIUS, depth), pl.ds(row, tall), :],
+            field.at[0, xc, pl.ds(RADIUS, depth), pl.ds(row, tall), :],
             first_hbm.at[0, :, pl.ds(pl.multiple_of(row - PAD, 8), tall), lanes(xc)],
             out_sem.at[16 + n * 4 + xc],
         )
@@ -448,6 +444,7 @@
 
             lax.fori_loop(RADIUS, depth - RADIUS, inner, 0)
             if t == 0:
+                spread_rows(c)
                 add_image(0, c, row, True)
             if t == 2:
 
@@ -479,16 +476,28 @@
 
                     lax.fori_loop(0, depth, plane, 0)
 
-            wait_halo(t, n)
-
-            def outer(z, carry):
-                update(t, c, row, z)
-                update(t, c, row, depth - RADIUS + z)
-                return carry
-
-            lax.fori_loop(0, RADIUS, outer, 0)
+            @pl.when(has_down)
+            def _():
+                halo_copy(t, n, 0).wait_recv()
+
+            lax.fori_loop(0, RADIUS, inner, 0)
             if t < STEPS - 1:
-                send_halo(t + 1, n)
+
+                @pl.when(has_down)
+                def _():
+                    halo_copy(t + 1, n, 1).start()
+
+            @pl.when(has_up)
+            def _():
+                halo_copy(t, n, 1).wait_recv()
+
+            lax.fori_loop(depth - RADIUS, depth, inner, 0)
+            if t < STEPS - 1:
+
+                @pl.when(has_up)
+                def _():
+                    halo_copy(t + 1, n, 0).start()
+
                 add_image(t + 1, c, row, False)
             else:
                 for xc in range(4):
@@ -510,7 +519,7 @@
         if t == 1:
             last = len(stages) - 1
             sum_copy(last).wait_recv()
-            sums[last + 1] = sums[last] + sums_in[last]
+            sums[last + 1] = (sums[last] + sums_in[last]) * scale
         if t == 2:
             for xc in range(4):
                 store(
@@ -544,6 +553,20 @@
     lax.fori_loop(0, CHUNKS, drain, 0)
     for copy in outs:
         copy.wait()
+
+
+def finish(g_in, f_in, s_in, m_in, g_out, f_out, s_out, m_out, tile, one, sem):
+    pairs = [(m_in, tile), (f_in, f_out), (s_in, s_out), (g_in, g_out)]
+    copies = [pltpu.make_async_copy(a, b, sem.at[i]) for i, (a, b) in enumerate(pairs)]
+    for copy in copies:
+        copy.start()
+    copies[0].wait()
+    one[...] = tile[0:1, 0:1]
+    last = pltpu.make_async_copy(one, m_out, sem.at[len(pairs)])
+    last.start()
+    for copy in copies[1:]:
+        copy.wait()
+    last.wait()
 
 
 def body(
@@ -566,9 +589,9 @@
     quarter = (4, depth, tall, LANES)
     stages = (space_size * shot_size).bit_length() - 1
     whole = pl.BlockSpec(memory_space=pl.ANY)
-    scalars = pl.BlockSpec(memory_space=pltpu.SMEM)
+    outside = pl.BlockSpec(memory_space=pltpu.HBM)
     f32 = jnp.float32
-    gradient, first, second, misfit = pl.pallas_call(
+    results = pl.pallas_call(
         functools.partial(kernel, space_size, shot_size),
         out_shape=(
             jax.ShapeDtypeStruct((depth, tall, width), f32),
@@ -576,10 +599,12 @@
             jax.ShapeDtypeStruct(adjoint_now.shape, f32),
             jax.ShapeDtypeStruct((8, LANES), f32),
         ),
-        in_specs=[scalars, scalars] + [whole] * 7,
+        in_specs=[outside] * 9,
         out_specs=[whole] * 4,
         scratch_shapes=[
-            pltpu.VMEM((STEPS + 2, 4, depth + 2 * RADIUS, height + 2 * PAD, LANES), f32),
+            pltpu.SMEM(scale_table.shape, f32),
+            pltpu.SMEM(source_cell.shape, jnp.int32),
+            pltpu.VMEM((STEPS + 1, 4, depth + 2 * RADIUS, height + 2 * PAD, LANES), f32),
             pltpu.VMEM((4, depth, height, LANES), f32),
             pltpu.VMEM((levels, depth, height, LANES), jnp.int32),
             pltpu.VMEM((levels, depth, 4 * height), jnp.int32),
@@ -609,21 +634,39 @@
             pltpu.SemaphoreType.DMA((stages,)),
         ],
         compiler_params=pltpu.CompilerParams(
-            collective_id=0, has_side_effects=True, vmem_limit_bytes=60 * 1024 * 1024
+            collective_id=0, has_side_effects=True, vmem_limit_bytes=48 * 1024 * 1024
         ),
     )(
-        scale_table,
-        source_cell[0],
-        adjoint_now,
-        adjoint_later,
-        courant,
-        checkpoint_codes,
-        scale_index,
-        receiver_cell,
-        observed,
+        *(
+            pltpu.with_memory_space_constraint(x, pltpu.HBM)
+            for x in (
+                adjoint_now,
+                adjoint_later,
+                courant,
+                checkpoint_codes,
+                scale_index,
+                receiver_cell,
+                observed,
+                scale_table,
+                source_cell,
+            )
+        )
     )
-    count = shot_size * STEPS * receivers * space_size
-    return gradient, first, second, 0.5 * misfit[0, 0] / count
+    gradient, first, second, misfit = pl.pallas_call(
+        finish,
+        out_shape=tuple(
+            jax.ShapeDtypeStruct(x.shape if i < 3 else (1, 1), f32) for i, x in enumerate(results)
+        ),
+        in_specs=[whole] * 4,
+        out_specs=[outside] * 4,
+        scratch_shapes=[
+            pltpu.VMEM((8, LANES), f32),
+            pltpu.VMEM((1, 1), f32),
+            pltpu.SemaphoreType.DMA((5,)),
+        ],
+        compiler_params=pltpu.CompilerParams(vmem_limit_bytes=1024 * 1024),
+    )(*results)
+    return gradient, first, second, misfit.reshape(())
 
 
 def solution(mesh):

time: 132 us -> 124 us (0.939); the launches traced: 131 us -> 121 us
  local copies, waits for them, and re-layouts: 7.68 us -> 0 us
  between operations: 2.43 us -> 0.64 us
    unnamed x5 -> x0, local copies, waits for them, and re-layouts: 6.5 us -> none
    pallas_call x1, Pallas kernels: 121 us -> 118 us  [body(): pl.pallas_call(functools.partial(kernel, space_size, shot_size), out_shap...]
    pallas_call x0 -> x1, Pallas kernels: none -> 2.22 us  [body(): pl.pallas_call(finish, out_shape=tuple((jax.ShapeDtypeStruct(x.shape if i...]
where the time goes in v2:
time: 124 us; the launch traced here: 121 us
  Pallas kernels  121 us (98%)
    pallas_call x1, Pallas kernels, body(): pl.pallas_call(functools.partial(kernel, space_size, shot_size), out_shap...  118 us

profile of v2, /device:TPU:2, one launch (start us, length us, event | category | flops | bytes accessed | tf_op | source)
XLA Modules:
  0.0 121.2 jit_solution(14671903930633473799)
XLA Ops:
  0.6 118.4 %shard_map.120 = (f32[16,16,512]{2,1,0:T(8,128)S(1)}, f32[1,16,64,512]{3,2,1,0:T(8,128)S(1)}, f32[1,16,64,512]{3,2,1,0:T(8,128)S(1)}, f32[8,128]{1,0:T(8,128)S(1)}) custom-call(f32[1,16,64,512]{3,2,1,0:T(8,128)} %now_hbm.1, f32[1,16,64,512]{3,2,1,0:T(8,128)} %later_hbm.1, f32[16,64,512]{2,1,0:T(8,128)} %courant_hbm.1, s32[1,6,16,64,128]{4,3,2,1,0:T(8,128)} %codes_hbm.1, ...), custom_call_target="tpu_custom_call" | custom-call | tf_op jit(solution)/shard_map/pallas_call | solution.py:594
  119.0 2.2 %shard_map.121 = (f32[16,16,512]{2,1,0:T(8,128)}, f32[1,16,64,512]{3,2,1,0:T(8,128)}, f32[1,16,64,512]{3,2,1,0:T(8,128)}, f32[1,1]{1,0:T(1,128)}) custom-call(f32[16,16,512]{2,1,0:T(8,128)S(1)} %get-tuple-element.12.g_in, f32[1,16,64,512]{3,2,1,0:T(8,128)S(1)} %get-tuple-element.13.f_in, f32[1,16,64,512]{3,2,1,0:T(8,128)S(1)} %get-tuple-element.14.s_in, ...), custom_call_target="tpu_custom_call" | custom-call | tf_op jit(solution)/shard_map/pallas_call | solution.py:655

commit v3 on v2

--- a/solution.py
+++ b/solution.py
@@ -48,6 +48,7 @@
     cols_hot,
     values,
     injected,
+    scale_at,
     image,
     from_sibling,
     combined,
@@ -240,14 +241,14 @@
     cols_hot[...] = jnp.where(col_ids == col_of, 1.0, 0.0).astype(jnp.bfloat16)
     block_ids = lax.broadcasted_iota(jnp.int32, (4 * height, receivers), 0)
     blocks_hot = jnp.where(block_ids == block_of, 1.0, 0.0)
-    scale_at = jnp.dot(
+    scale_at[...] = jnp.dot(
         scales[...], blocks_hot, precision=lax.Precision.HIGHEST, preferred_element_type=jnp.float32
     )
     depth_ids = lax.broadcasted_iota(jnp.int32, (depth, receivers), 0)
     small_words.wait()
     planes = 4
-    total = jnp.zeros((1, receivers), jnp.float32)
-    for t in range(STEPS):
+
+    def residuals(t):
         level = STEPS - t
 
         def gather(i, acc):
@@ -262,21 +263,21 @@
             hot = rows_hot[pl.ds(i * planes, planes), :, :].reshape(planes * height, receivers)
             return acc + jnp.sum(found * hot.astype(jnp.float32), axis=0, keepdims=True)
 
-        code = lax.fori_loop(
-            0, depth // planes, gather, jnp.zeros((1, receivers), jnp.float32)
-        )
-        part = scale_at[level * depth : (level + 1) * depth]
+        code = lax.fori_loop(0, depth // planes, gather, jnp.zeros((1, receivers), jnp.float32))
+        part = scale_at[pl.ds(level * depth, depth), :]
         factor = jnp.sum(jnp.where(depth_ids == slab_of, part, 0.0), axis=0, keepdims=True)
         residual = code * factor - observed[level - 1 : level, :]
-        total = total + residual * residual
+        squares = jnp.broadcast_to(
+            jnp.sum(residual * residual, axis=1, keepdims=True), sums.shape[1:]
+        )
+        sums[0] = squares if t == 0 else sums[0] + squares
         left = residual
         for piece in range(3):
             short = left.astype(jnp.bfloat16).astype(jnp.float32)
             left = left - short
             values[t, piece] = jnp.where(col_ids == col_of, short, 0.0).astype(jnp.bfloat16)
-    sums[0] = jnp.broadcast_to(
-        jnp.sum(total, axis=1, keepdims=True), sums.shape[1:]
-    )
+
+    residuals(0)
 
     def sum_copy(b):
         return pltpu.make_async_remote_copy(
@@ -425,9 +426,9 @@
 
         def task(n, carry, t=t):
             c, row = rows_of(n)
-            if t < 2:
+            if t in (1, 2):
                 for j in range(4):
-                    b = 4 * t + j
+                    b = 4 * (t - 1) + j
 
                     @pl.when(n == j)
                     def _():
@@ -443,12 +444,9 @@
                 return carry
 
             lax.fori_loop(RADIUS, depth - RADIUS, inner, 0)
-            if t == 0:
-                spread_rows(c)
-                add_image(0, c, row, True)
-            if t == 2:
-
-                @pl.when(n == 2)
+            if t == 3:
+
+                @pl.when(n == 0)
                 def _():
                     far_copy.wait_recv()
 
@@ -460,22 +458,6 @@
                     lax.fori_loop(0, depth, plane, 0)
                     partner_copy.start()
 
-            if t == 3:
-
-                @pl.when(n == 3)
-                def _():
-                    near_copy.wait_recv()
-                    partner_copy.wait_recv()
-
-                    def plane(z, carry):
-                        for m in range(4):
-                            grad_out[m, z] = (
-                                image[near, m, z] + from_sibling[1, m, z] + from_partner[m, z]
-                            )
-                        return carry
-
-                    lax.fori_loop(0, depth, plane, 0)
-
             @pl.when(has_down)
             def _():
                 halo_copy(t, n, 0).wait_recv()
@@ -498,8 +480,21 @@
                 def _():
                     halo_copy(t + 1, n, 0).start()
 
-                add_image(t + 1, c, row, False)
-            else:
+            if t == 0:
+                for j in range(1, STEPS):
+
+                    @pl.when(n == j - 1)
+                    def _():
+                        residuals(j)
+
+            if t == 1:
+                spread_rows(c)
+                add_image(0, c, row, True)
+                add_image(1, c, row, False)
+            if t == 2:
+                add_image(2, c, row, False)
+                add_image(3, c, row, False)
+            if t == STEPS - 1:
                 for xc in range(4):
                     first_copy(n, xc).start()
             if t == 2:
@@ -516,7 +511,7 @@
             return carry
 
         lax.fori_loop(0, CHUNKS, task, 0)
-        if t == 1:
+        if t == 2:
             last = len(stages) - 1
             sum_copy(last).wait_recv()
             sums[last + 1] = (sums[last] + sums_in[last]) * scale
@@ -527,6 +522,17 @@
                     second_hbm.at[0, :, :, lanes(xc)],
                 )
             store(sums.at[len(stages)], misfit_hbm)
+    near_copy.wait_recv()
+    partner_copy.wait_recv()
+
+    def plane(z, carry):
+        for m in range(4):
+            grad_out[m, z] = (
+                image[near, m, z] + from_sibling[1, m, z] + from_partner[m, z]
+            )
+        return carry
+
+    lax.fori_loop(0, depth, plane, 0)
     for xc in range(4):
         store(grad_out.at[xc], grad_hbm.at[:, :, lanes(xc)])
 
@@ -617,6 +623,7 @@
             pltpu.VMEM((width, receivers), jnp.bfloat16),
             pltpu.VMEM((STEPS, 3, width, receivers), jnp.bfloat16),
             pltpu.VMEM(quarter, f32),
+            pltpu.VMEM((LANES, receivers), f32),
             pltpu.VMEM((CHUNKS, *quarter), f32),
             pltpu.VMEM((2, *quarter), f32),
             pltpu.VMEM(quarter, f32),

time: 124 us -> 119 us (0.960); the launches traced: 121 us -> 118 us
  Pallas kernels: 121 us -> 118 us
    pallas_call x1, Pallas kernels: 118 us -> 115 us  [body(): pl.pallas_call(functools.partial(kernel, space_size, shot_size), out_shap...]
where the time goes in v3:
time: 119 us; the launch traced here: 118 us
  Pallas kernels  118 us (99%)
    pallas_call x1, Pallas kernels, body(): pl.pallas_call(functools.partial(kernel, space_size, shot_size), out_shap...  115 us

profile of v3, /device:TPU:2, one launch (start us, length us, event | category | flops | bytes accessed | tf_op | source)
XLA Modules:
  0.0 118.2 jit_solution(10213293816586422634)
XLA Ops:
  0.6 115.3 %shard_map.120 = (f32[16,16,512]{2,1,0:T(8,128)S(1)}, f32[1,16,64,512]{3,2,1,0:T(8,128)S(1)}, f32[1,16,64,512]{3,2,1,0:T(8,128)S(1)}, f32[8,128]{1,0:T(8,128)S(1)}) custom-call(f32[1,16,64,512]{3,2,1,0:T(8,128)} %now_hbm.1, f32[1,16,64,512]{3,2,1,0:T(8,128)} %later_hbm.1, f32[16,64,512]{2,1,0:T(8,128)} %courant_hbm.1, s32[1,6,16,64,128]{4,3,2,1,0:T(8,128)} %codes_hbm.1, ...), custom_call_target="tpu_custom_call" | custom-call | tf_op jit(solution)/shard_map/pallas_call | solution.py:600
  115.9 2.2 %shard_map.121 = (f32[16,16,512]{2,1,0:T(8,128)}, f32[1,16,64,512]{3,2,1,0:T(8,128)}, f32[1,16,64,512]{3,2,1,0:T(8,128)}, f32[1,1]{1,0:T(1,128)}) custom-call(f32[16,16,512]{2,1,0:T(8,128)S(1)} %get-tuple-element.12.g_in, f32[1,16,64,512]{3,2,1,0:T(8,128)S(1)} %get-tuple-element.13.f_in, f32[1,16,64,512]{3,2,1,0:T(8,128)S(1)} %get-tuple-element.14.s_in, ...), custom_call_target="tpu_custom_call" | custom-call | tf_op jit(solution)/shard_map/pallas_call | solution.py:662

commit v4 on v3

--- a/solution.py
+++ b/solution.py
@@ -56,6 +56,8 @@
     grad_out,
     sums,
     sums_in,
+    gathered,
+    ordered,
     load_sem,
     out_sem,
     halo_send,
@@ -64,6 +66,7 @@
     image_recv,
     sum_send,
     sum_recv,
+    met,
 ):
     scale = 0.5 / (shot_size * STEPS * cells.shape[1] * space_size)
     depth = courant.shape[1]
@@ -77,22 +80,20 @@
     sibling = shot + 1 - 2 * core
     partner = (shot + 2) % 4
 
-    def flip(i, bit):
-        return i + bit - 2 * bit * ((i // bit) % 2)
-
-    stages = []
-    bit = 1
-    while bit < space_size:
-        stages.append({"space": flip(me, bit)})
-        bit *= 2
-    bit = 1
-    while bit < shot_size:
-        stages.append({"shot": flip(shot, bit)})
-        bit *= 2
-    peers = stages + [{"space": up}, {"space": down}]
+    peers = [{"space": up}, {"space": down}, {"shot": sibling}, {"shot": partner}]
     barrier = pltpu.get_barrier_semaphore()
     for peer in peers:
         pl.semaphore_signal(barrier, inc=1, device_id=peer, device_id_type=MESH)
+
+    stages = [{"shot": sibling}, {"shot": partner}]
+    hello = [None, None]
+    windows = [None, None]
+    bit = 1
+    while bit < space_size:
+        stages.append({"space": (me + bit) % space_size})
+        hello.append({"space": (me + space_size - bit) % space_size})
+        windows.append(bit)
+        bit *= 2
 
     loads = []
 
@@ -279,10 +280,21 @@
 
     residuals(0)
 
+    def end_stage(b):
+        sum_copy(b).wait_recv()
+        if hello[b] is not None:
+            pl.semaphore_wait(met.at[b], 1)
+        else:
+            both = sums[b] + sums_in[b]
+            sums[b + 1] = both
+            if windows[b + 1] is not None:
+                gathered[0] = both[0:1]
+
     def sum_copy(b):
+        bit = windows[b]
         return pltpu.make_async_remote_copy(
-            src_ref=sums.at[b],
-            dst_ref=sums_in.at[b],
+            src_ref=sums.at[b] if bit is None else gathered.at[pl.ds(0, bit)],
+            dst_ref=sums_in.at[b] if bit is None else gathered.at[pl.ds(bit, bit)],
             send_sem=sum_send.at[b],
             recv_sem=sum_recv.at[b],
             device_id=stages[b],
@@ -433,9 +445,12 @@
                     @pl.when(n == j)
                     def _():
                         if b > 0:
-                            sum_copy(b - 1).wait_recv()
-                            sums[b] = sums[b - 1] + sums_in[b - 1]
+                            end_stage(b - 1)
                         sum_copy(b).start()
+                        if hello[b] is not None:
+                            pl.semaphore_signal(
+                                met.at[b], inc=1, device_id=hello[b], device_id_type=MESH
+                            )
 
             inject(t, c)
 
@@ -513,15 +528,22 @@
         lax.fori_loop(0, CHUNKS, task, 0)
         if t == 2:
             last = len(stages) - 1
-            sum_copy(last).wait_recv()
-            sums[last + 1] = (sums[last] + sums_in[last]) * scale
+            end_stage(last)
+
+            def place(k, carry):
+                ordered[pl.ds((me + space_size - k) % space_size, 1)] = gathered[pl.ds(k, 1)]
+                return carry
+
+            lax.fori_loop(0, space_size, place, 0)
+            everyone = jnp.sum(ordered[...], axis=0) * scale
+            sums[3] = jnp.broadcast_to(everyone, sums.shape[1:])
         if t == 2:
             for xc in range(4):
                 store(
                     field.at[STEPS, xc, pl.ds(RADIUS, depth), pl.ds(PAD, height), :],
                     second_hbm.at[0, :, :, lanes(xc)],
                 )
-            store(sums.at[len(stages)], misfit_hbm)
+            store(sums.at[3], misfit_hbm)
     near_copy.wait_recv()
     partner_copy.wait_recv()
 
@@ -629,8 +651,10 @@
             pltpu.VMEM(quarter, f32),
             pltpu.VMEM(quarter, f32),
             pltpu.VMEM(quarter, f32),
-            pltpu.VMEM((stages + 1, 8, LANES), f32),
-            pltpu.VMEM((stages, 8, LANES), f32),
+            pltpu.VMEM((4, 8, LANES), f32),
+            pltpu.VMEM((2, 8, LANES), f32),
+            pltpu.VMEM((space_size, 1, LANES), f32),
+            pltpu.VMEM((space_size, 1, LANES), f32),
             pltpu.SemaphoreType.DMA((32,)),
             pltpu.SemaphoreType.DMA((32,)),
             pltpu.SemaphoreType.DMA((2, STEPS, CHUNKS)),
@@ -639,6 +663,7 @@
             pltpu.SemaphoreType.DMA((3,)),
             pltpu.SemaphoreType.DMA((stages,)),
             pltpu.SemaphoreType.DMA((stages,)),
+            pltpu.SemaphoreType.REGULAR((stages,)),
         ],
         compiler_params=pltpu.CompilerParams(
             collective_id=0, has_side_effects=True, vmem_limit_bytes=48 * 1024 * 1024

time: 119 us -> 116 us (0.975); the launches traced: 118 us -> 114 us
  Pallas kernels: 118 us -> 113 us
    pallas_call x1, Pallas kernels: 115 us -> 111 us  [body(): pl.pallas_call(functools.partial(kernel, space_size, shot_size), out_shap...]
where the time goes in v4:
time: 116 us; the launch traced here: 114 us
  Pallas kernels  113 us (97%)
    pallas_call x1, Pallas kernels, body(): pl.pallas_call(functools.partial(kernel, space_size, shot_size), out_shap...  111 us

profile of v4, /device:TPU:2, one launch (start us, length us, event | category | flops | bytes accessed | tf_op | source)
XLA Modules:
  0.0 114.0 jit_solution(5788107388511009591)
XLA Ops:
  0.6 111.1 %shard_map.120 = (f32[16,16,512]{2,1,0:T(8,128)S(1)}, f32[1,16,64,512]{3,2,1,0:T(8,128)S(1)}, f32[1,16,64,512]{3,2,1,0:T(8,128)S(1)}, f32[8,128]{1,0:T(8,128)S(1)}) custom-call(f32[1,16,64,512]{3,2,1,0:T(8,128)} %now_hbm.1, f32[1,16,64,512]{3,2,1,0:T(8,128)} %later_hbm.1, f32[16,64,512]{2,1,0:T(8,128)} %courant_hbm.1, s32[1,6,16,64,128]{4,3,2,1,0:T(8,128)} %codes_hbm.1, ...), custom_call_target="tpu_custom_call" | custom-call | tf_op jit(solution)/shard_map/pallas_call | solution.py:622
  111.7 2.2 %shard_map.121 = (f32[16,16,512]{2,1,0:T(8,128)}, f32[1,16,64,512]{3,2,1,0:T(8,128)}, f32[1,16,64,512]{3,2,1,0:T(8,128)}, f32[1,1]{1,0:T(1,128)}) custom-call(f32[16,16,512]{2,1,0:T(8,128)S(1)} %get-tuple-element.12.g_in, f32[1,16,64,512]{3,2,1,0:T(8,128)S(1)} %get-tuple-element.13.f_in, f32[1,16,64,512]{3,2,1,0:T(8,128)S(1)} %get-tuple-element.14.s_in, ...), custom_call_target="tpu_custom_call" | custom-call | tf_op jit(solution)/shard_map/pallas_call | solution.py:687

commit v5 on v4

--- a/solution.py
+++ b/solution.py
@@ -410,14 +410,17 @@
     sibling_far = 2 * (1 - side) + 1 - core
     far_copy = pair_copy(sibling_far, 0)
     near_copy = pair_copy(sibling, 1)
-    partner_copy = pltpu.make_async_remote_copy(
-        src_ref=combined,
-        dst_ref=from_partner,
-        send_sem=image_send.at[2],
-        recv_sem=image_recv.at[2],
-        device_id={"shot": partner},
-        device_id_type=MESH,
-    )
+    partner_copies = [
+        pltpu.make_async_remote_copy(
+            src_ref=combined.at[m],
+            dst_ref=from_partner.at[m],
+            send_sem=image_send.at[2 + m],
+            recv_sem=image_recv.at[2 + m],
+            device_id={"shot": partner},
+            device_id_type=MESH,
+        )
+        for m in range(4)
+    ]
 
     outs = []
 
@@ -471,7 +474,8 @@
                         return carry
 
                     lax.fori_loop(0, depth, plane, 0)
-                    partner_copy.start()
+                    for copy in partner_copies:
+                        copy.start()
 
             @pl.when(has_down)
             def _():
@@ -545,18 +549,15 @@
                 )
             store(sums.at[3], misfit_hbm)
     near_copy.wait_recv()
-    partner_copy.wait_recv()
-
-    def plane(z, carry):
-        for m in range(4):
-            grad_out[m, z] = (
-                image[near, m, z] + from_sibling[1, m, z] + from_partner[m, z]
-            )
-        return carry
-
-    lax.fori_loop(0, depth, plane, 0)
-    for xc in range(4):
-        store(grad_out.at[xc], grad_hbm.at[:, :, lanes(xc)])
+    for m in range(4):
+        partner_copies[m].wait_recv()
+
+        def plane(z, carry, m=m):
+            grad_out[m, z] = image[near, m, z] + from_sibling[1, m, z] + from_partner[m, z]
+            return carry
+
+        lax.fori_loop(0, depth, plane, 0)
+        store(grad_out.at[m], grad_hbm.at[:, :, lanes(m)])
 
     def drain(n, carry):
         for t in range(STEPS):
@@ -575,7 +576,8 @@
 
     far_copy.wait_send()
     near_copy.wait_send()
-    partner_copy.wait_send()
+    for copy in partner_copies:
+        copy.wait_send()
     for b in range(len(stages)):
         sum_copy(b).wait_send()
     lax.fori_loop(0, CHUNKS, drain, 0)
@@ -584,7 +586,12 @@
 
 
 def finish(g_in, f_in, s_in, m_in, g_out, f_out, s_out, m_out, tile, one, sem):
-    pairs = [(m_in, tile), (f_in, f_out), (s_in, s_out), (g_in, g_out)]
+    quarter = f_in.shape[1] // 4
+    pairs = [(m_in, tile), (g_in, g_out)] + [
+        (a.at[0, pl.ds(i * quarter, quarter)], b.at[0, pl.ds(i * quarter, quarter)])
+        for a, b in ((f_in, f_out), (s_in, s_out))
+        for i in range(4)
+    ]
     copies = [pltpu.make_async_copy(a, b, sem.at[i]) for i, (a, b) in enumerate(pairs)]
     for copy in copies:
         copy.start()
@@ -659,8 +666,8 @@
             pltpu.SemaphoreType.DMA((32,)),
             pltpu.SemaphoreType.DMA((2, STEPS, CHUNKS)),
             pltpu.SemaphoreType.DMA((2, STEPS, CHUNKS)),
-            pltpu.SemaphoreType.DMA((3,)),
-            pltpu.SemaphoreType.DMA((3,)),
+            pltpu.SemaphoreType.DMA((6,)),
+            pltpu.SemaphoreType.DMA((6,)),
             pltpu.SemaphoreType.DMA((stages,)),
             pltpu.SemaphoreType.DMA((stages,)),
             pltpu.SemaphoreType.REGULAR((stages,)),
@@ -694,7 +701,7 @@
         scratch_shapes=[
             pltpu.VMEM((8, LANES), f32),
             pltpu.VMEM((1, 1), f32),
-            pltpu.SemaphoreType.DMA((5,)),
+            pltpu.SemaphoreType.DMA((11,)),
         ],
         compiler_params=pltpu.CompilerParams(vmem_limit_bytes=1024 * 1024),
     )(*results)

time: 116 us -> 116 us (level)
  no operation moved by 1% of the time
where the time goes in v5:
time: 116 us; the launch traced here: 114 us
  Pallas kernels  113 us (97%)
    pallas_call x1, Pallas kernels, body(): pl.pallas_call(functools.partial(kernel, space_size, shot_size), out_shap...  111 us

profile of v5, /device:TPU:2, one launch (start us, length us, event | category | flops | bytes accessed | tf_op | source)
XLA Modules:
  0.0 114.0 jit_solution(17102305874512040268)
XLA Ops:
  0.6 111.0 %shard_map.120 = (f32[16,16,512]{2,1,0:T(8,128)S(1)}, f32[1,16,64,512]{3,2,1,0:T(8,128)S(1)}, f32[1,16,64,512]{3,2,1,0:T(8,128)S(1)}, f32[8,128]{1,0:T(8,128)S(1)}) custom-call(f32[1,16,64,512]{3,2,1,0:T(8,128)} %now_hbm.1, f32[1,16,64,512]{3,2,1,0:T(8,128)} %later_hbm.1, f32[16,64,512]{2,1,0:T(8,128)} %courant_hbm.1, s32[1,6,16,64,128]{4,3,2,1,0:T(8,128)} %codes_hbm.1, ...), custom_call_target="tpu_custom_call" | custom-call | tf_op jit(solution)/shard_map/pallas_call | solution.py:629
  111.7 2.3 %shard_map.121 = (f32[16,16,512]{2,1,0:T(8,128)}, f32[1,16,64,512]{3,2,1,0:T(8,128)}, f32[1,16,64,512]{3,2,1,0:T(8,128)}, f32[1,1]{1,0:T(1,128)}) custom-call(f32[16,16,512]{2,1,0:T(8,128)S(1)} %get-tuple-element.12.g_in, f32[1,16,64,512]{3,2,1,0:T(8,128)S(1)} %get-tuple-element.13.f_in, f32[1,16,64,512]{3,2,1,0:T(8,128)S(1)} %get-tuple-element.14.s_in, ...), custom_call_target="tpu_custom_call" | custom-call | tf_op jit(solution)/shard_map/pallas_call | solution.py:694
